TPU v7x, 128 devices: a whole 4x4x4 slice. The times are simulated.
128 devices in a mesh: runs: 32 (over z, y, core), tp: 4 (over x).
Axes of the slice: x: 4, y: 4, z: 4, core: 2. Of those that a mesh axis runs over, the one named last changes fastest.
Arguments:
- hidden: bfloat16 [16384, 8192], P('runs', 'tp'), may hold values from -6 to 6
- cotangent: bfloat16 [16384, 8192], P('runs', 'tp'), may hold values from -0.059814453 to 0.059814453
- rotation: float32 [8192, 512], P(None, 'tp'), may hold values from -0.0625 to 0.0625
- matching: int32 [128], P('runs'), may hold values from 0 to 127
- mask: int32 [128, 128], P('runs'), may hold values 0 or 1
Outputs:
- intervened: bfloat16 [16384, 8192], P('runs', 'tp')
- grad_rotation: float32 [8192, 512], P('runs', 'tp')
All inputs are finite; a program needn't handle non-finite values. No bound on the sum of `mask` on one device may be relied on, other than what follows from the above.
Results may differ from a plain program's by a relative error of at most 0.0045.
Values may be sent and summed in bfloat16 or wider, within the bound.
No kernel may reach another device: no remote copies, remote signals or barrier semaphores. Data moves between devices by JAX's collectives and lax.ppermute only.
A program may use at most 128 MiB of HBM per device.

v0:
```python
import jax
import jax.numpy as jnp
from jax import lax
from jax.experimental import pallas as pl
from jax.experimental.pallas import tpu as pltpu
from jax.sharding import PartitionSpec as P


Z, Y, CORES, TP = 4, 4, 2, 4
bf16, f32 = jnp.bfloat16, jnp.float32
ORDER = (1, 3, 2)
STRETCHES = 2
VMEM = pl.BlockSpec(memory_space=pltpu.VMEM)
SMEM = pl.BlockSpec(memory_space=pltpu.SMEM)


def along_runs(dz, dy, dcore):
    return [
        (z * 8 + y * 2 + c, (z + dz) % Z * 8 + (y + dy) % Y * 2 + (c + dcore) % CORES)
        for z in range(Z)
        for y in range(Y)
        for c in range(CORES)
    ]


def along_tp(dx):
    return [(x, (x + dx) % TP) for x in range(TP)]


def shift_tp(value, dx):
    return lax.ppermute(value, "tp", along_tp(dx)) if dx % TP else value


def shift_y(value, dy):
    return lax.ppermute(value, "runs", along_runs(0, dy, 0)) if dy % Y else value


def by_core(value, first, second):
    pairs = along_runs(*first, 0)[0::2] + along_runs(*second, 0)[1::2]
    return lax.ppermute(value, "runs", pairs)


def swap_cores(value):
    return lax.ppermute(value, "runs", along_runs(0, 0, 1))


def ordered(send):
    sent = {k: send(k) for k in ORDER}
    return [sent[k] for k in sorted(sent)]


def dot(a, b, dims=((1,), (0,))):
    return lax.dot_general(a, b, (dims, ((), ())), preferred_element_type=f32)


def kernel(body, outs, scalars, arrays, flops=0, scratch=(), grant=16):
    call = pl.pallas_call(
        body,
        out_shape=[jax.ShapeDtypeStruct(shape, dtype) for shape, dtype in outs],
        in_specs=[SMEM] * len(scalars) + [VMEM] * len(arrays),
        out_specs=[VMEM] * len(outs),
        scratch_shapes=list(scratch),
        compiler_params=pltpu.CompilerParams(vmem_limit_bytes=grant << 20),
        cost_estimate=pl.CostEstimate(flops=flops, bytes_accessed=0, transcendentals=0)
        if flops
        else None,
    )
    return call(*scalars, *arrays)


def stretched(value, length):
    each = length // STRETCHES
    starts = range(0, value.shape[0], length)
    return [
        jnp.concatenate([value[at + part * each : at + (part + 1) * each] for at in starts])
        for part in range(STRETCHES)
    ]


def joined(parts, length):
    each = length // STRETCHES
    starts = range(0, parts[0].shape[0], each)
    return jnp.concatenate([part[at : at + each] for at in starts for part in parts])


def own_products(hidden, cotangent, own, length):
    tokens = hidden.shape[0]
    shape = (tokens // STRETCHES, own.shape[1])

    def body(hidden_ref, cotangent_ref, own_ref, rounded, *outs):
        high = own_ref[...].astype(bf16)
        low = (own_ref[...] - high.astype(f32)).astype(bf16)
        rounded[...] = high
        both = jnp.concatenate([high, low], axis=1)
        for i, left in enumerate((hidden_ref, cotangent_ref)):
            total = dot(left[...], both)
            total = total[:, : shape[1]] + total[:, shape[1] :]
            for part, pieces in enumerate(stretched(total, length)):
                outs[i * STRETCHES + part][...] = pieces

    outs = kernel(
        body,
        [(own.shape, bf16)] + [(shape, f32)] * 2 * STRETCHES,
        [],
        [hidden, cotangent, own],
        flops=8 * tokens * own.shape[0] * own.shape[1],
    )
    return outs[0], list(outs[1 : 1 + STRETCHES]), list(outs[1 + STRETCHES :])


def partial_products(core, hidden, cotangent, near, far, length):
    tokens, features = hidden.shape
    half, columns = near[0].shape
    count = len(near)

    rows = 2 * tokens // STRETCHES

    def body(core_ref, hidden_ref, cotangent_ref, *refs):
        ins, outs = refs[: 2 * count], refs[2 * count :]
        at = pl.multiple_of(core_ref[0] * half, half)
        past = pl.multiple_of((1 - core_ref[0]) * half, half)
        here = jnp.concatenate([value[...] for value in ins[:count]], axis=1)
        there = jnp.concatenate([value[...] for value in ins[count:]], axis=1)
        for i, left in enumerate((hidden_ref, cotangent_ref)):
            total = dot(left[:, pl.ds(at, half)], here) + dot(left[:, pl.ds(past, half)], there)
            for part, pieces in enumerate(stretched(total.astype(bf16), length)):
                for k in range(count):
                    place = slice(i * rows // 2, (i + 1) * rows // 2)
                    outs[part * count + k][place] = pieces[:, k * columns : (k + 1) * columns]

    outs = kernel(
        body,
        [((rows, columns), bf16)] * count * STRETCHES,
        [core],
        [hidden, cotangent, *near, *far],
        flops=4 * tokens * features * columns * count,
    )
    return [outs[part * count : (part + 1) * count] for part in range(STRETCHES)]


def summed(core, coords, pulled, parts, chosen):
    tokens, columns = coords.shape

    def body(core_ref, coords_ref, pulled_ref, chosen_ref, *refs):
        ins, (own, taken, keep, give) = refs[: TP - 1], refs[TP - 1 :]
        total, other = coords_ref[...], pulled_ref[...]
        for value in ins:
            total = total + value[:tokens].astype(f32)
            other = other + value[tokens:].astype(f32)
        other = other * chosen_ref[...]
        own[...], taken[...] = total, other
        first = core_ref[0] == 0
        keep[...] = jnp.where(first, total, other).astype(bf16)
        give[...] = jnp.where(first, other, total).astype(bf16)

    shape = (tokens, columns)
    return kernel(
        body,
        [(shape, f32), (shape, f32), (shape, bf16), (shape, bf16)],
        [core],
        [coords, pulled, chosen, *parts],
    )


def copied(value):
    def body(value_ref, out):
        out[...] = value_ref[...]

    return kernel(body, [(value.shape, value.dtype)], [], [value])[0]


def both_cores(core, keep, got):
    tokens, columns = keep.shape

    def body(core_ref, keep_ref, got_ref, out):
        out[pl.ds(pl.multiple_of(core_ref[0] * tokens, tokens), tokens)] = keep_ref[...]
        out[pl.ds(pl.multiple_of((1 - core_ref[0]) * tokens, tokens), tokens)] = got_ref[...]

    return kernel(body, [((2 * tokens, columns), bf16)], [core], [keep, got])[0]


def route_runs(core, index, parts, length):
    shape = parts[0].shape
    each = shape[0] // length
    slots = each * Z

    def body(core_ref, index_ref, *refs):
        ins, outs, (wide, packed, held) = refs[:Z], refs[Z : 2 * Z], refs[2 * Z :]

        @pl.when(core_ref[0] == 0)
        def _():
            for k, part in enumerate(ins):
                packed[k * shape[0] : (k + 1) * shape[0]] = part[...]
            for k, out in enumerate(outs):
                for i in range(each):
                    at = pl.multiple_of(index_ref[each * k + i] * length, length)
                    out[i * length : (i + 1) * length] = packed[pl.ds(at, length)]
            wide[...] = jnp.zeros_like(wide)

        @pl.when(core_ref[0] != 0)
        def _():
            held[...] = jnp.zeros_like(held)
            for k, part in enumerate(ins):
                for i in range(each):
                    at = pl.multiple_of(index_ref[each * k + i] * length, length)
                    at = pl.ds(at, length)
                    held[at] = held[at] + part[i * length : (i + 1) * length].astype(f32)
            for k, out in enumerate(outs):
                out[...] = held[k * shape[0] : (k + 1) * shape[0]].astype(bf16)
            wide[...] = held[: shape[0]]

    return kernel(
        body,
        [(shape, bf16)] * Z + [(shape, f32)],
        [core, index],
        parts,
        scratch=[
            pltpu.VMEM((slots * length, shape[1]), bf16),
            pltpu.VMEM(((slots + 1) * length, shape[1]), f32),
        ],
    )


def finished_runs(core, from_row, wide, parts, length):
    rows, columns = wide.shape
    half = rows // 2

    def body(core_ref, from_ref, wide_ref, *refs):
        ins, (keep, give) = refs[:Z], refs[Z:]

        @pl.when(core_ref[0] == 0)
        def _():
            for i in range(rows // length):
                at = slice(i * length, (i + 1) * length)
                source = from_ref[i]
                picked = ins[0][at]
                for k in range(1, Y):
                    picked = jnp.where(source == k, ins[k][at], picked)
                out = keep if i * length < half else give
                out[i * length % half : i * length % half + length] = picked.astype(f32)

        @pl.when(core_ref[0] != 0)
        def _():
            total = wide_ref[...]
            for value in ins[1:]:
                total = total + value[...].astype(f32)
            give[...], keep[...] = total[:half], total[half:]

    shape = (half, columns)
    return kernel(body, [(shape, f32)] * 2, [core, from_row], [wide, *parts])


def update_and_net(core, keep, got, own, chosen, taken):
    tokens, columns = own.shape

    def body(core_ref, keep_ref, got_ref, own_ref, chosen_ref, taken_ref, out):
        first = core_ref[0] == 0
        picked = jnp.where(first, keep_ref[...], got_ref[...])
        returned = jnp.where(first, got_ref[...], keep_ref[...])
        out[:tokens] = (chosen_ref[...] * (picked - own_ref[...])).astype(bf16)
        out[tokens:] = (returned - taken_ref[...]).astype(bf16)

    return kernel(
        body, [((2 * tokens, columns), bf16)], [core], [keep, got, own, chosen, taken]
    )[0]


def gradient_rows(core, cotangent, hidden, gathered, length):
    tokens, features = hidden.shape
    rows = features // (Y * CORES)
    columns = gathered[0][0].shape[1]
    half = tokens // STRETCHES

    def body(core_ref, cotangent_ref, hidden_ref, *refs):
        ins, out = refs[:-1], refs[-1]
        ins = [
            jnp.concatenate([value[...] for value in ins[at : at + TP]], axis=1)
            for at in range(0, TP * STRETCHES, TP)
        ]
        update = joined([value[:half] for value in ins], length)
        net = joined([value[half:] for value in ins], length)
        for y in range(Y):
            at = pl.ds(pl.multiple_of((y * CORES + core_ref[0]) * rows, rows), rows)
            block = dot(cotangent_ref[:, at], update, ((0,), (0,)))
            block = block + dot(hidden_ref[:, at], net, ((0,), (0,)))
            for k in range(TP):
                place = (k * Y + y) * rows
                out[place : place + rows] = block[:, k * columns : (k + 1) * columns]

    return kernel(
        body,
        [((TP * Y * rows, columns), f32)],
        [core],
        [cotangent, hidden, *sum(gathered, [])],
        flops=2 * tokens * features * columns * TP,
    )[0]


def intervention(core, hidden, gathered, own_block, near, far, length):
    tokens, features = hidden.shape
    half = features // 2
    count = TP * STRETCHES
    rows_each = tokens // STRETCHES

    def body(core_ref, hidden_ref, own_ref, *refs):
        ins, rest, out = refs[:count], refs[count:-1], refs[-1]
        ins = [
            jnp.concatenate([value[:rows_each] for value in ins[at : at + TP]], axis=1)
            for at in range(0, count, TP)
        ]
        update = joined(ins, length)
        for which, pieces in enumerate((rest[: TP - 1], rest[TP - 1 :])):
            place = core_ref[0] if which == 0 else 1 - core_ref[0]
            at = pl.ds(pl.multiple_of(place * half, half), half)
            rows = jnp.concatenate([own_ref[at]] + [value[...] for value in pieces], axis=1)
            added = dot(update, rows, ((1,), (1,)))
            out[:, at] = (hidden_ref[:, at].astype(f32) + added).astype(bf16)

    return kernel(
        body,
        [((tokens, features), bf16)],
        [core],
        [hidden, own_block, *sum(gathered, []), *near, *far],
        flops=2 * tokens * features * own_block.shape[1] * TP,
    )[0]


def per_device(hidden, cotangent, rotation, matching, mask):
    _, features = hidden.shape
    local_runs, length = mask.shape
    columns = rotation.shape[1]
    half = features // 2
    x, run_at = lax.axis_index("tp"), lax.axis_index("runs")
    z, y, core = run_at // 8, run_at // 2 % Y, run_at % CORES
    this_core, other_core = core[None], 1 - core[None]

    near = []
    for k in ORDER:
        start = (x + k) % TP * features + core * half
        part = lax.dynamic_slice(rotation, (start, 0), (half, columns)).astype(bf16)
        near.append(shift_tp(part, k))
    far = [swap_cores(value) for value in near]
    own_wide = lax.dynamic_slice(rotation, (x * features, 0), (features, columns))
    own_block, coords, pulled = own_products(hidden, cotangent, own_wide, length)

    own_runs = run_at * local_runs + jnp.arange(local_runs, dtype=jnp.int32)
    chosen = (mask * (matching != own_runs)[:, None].astype(jnp.int32)).astype(f32)
    chosen = jnp.broadcast_to(chosen[:, :, None], (local_runs, length, columns))
    each = length // STRETCHES
    chosen = [
        chosen[:, part * each : (part + 1) * each].reshape(local_runs * each, columns)
        for part in range(STRETCHES)
    ]

    chosen[0] = copied(chosen[0])

    matching, pulled[0] = lax.optimization_barrier((matching, pulled[0]))
    other_matching = swap_cores(matching)
    chip_match = jnp.concatenate(
        [
            jnp.where(core == 0, matching, other_matching),
            jnp.where(core == 0, other_matching, matching),
        ]
    )
    column_match = [shift_y(chip_match, -k) for k in range(Y)]

    chip_runs = local_runs * CORES

    def slots(match):
        return (z - match // (chip_runs * Y)) % Z * chip_runs + match % chip_runs

    asked = jnp.concatenate([slots(match) for match in column_match])
    targets = jnp.concatenate(
        [
            jnp.where(match // chip_runs % Y == y, slots(match), Z * chip_runs)
            for match in (column_match[-k % Y] for k in range(Y))
        ]
    )
    index = jnp.where(core == 0, asked, targets)
    from_row = (y - chip_match // chip_runs) % Y

    parts = partial_products(this_core, hidden, cotangent, near, far, length)
    for part in range(STRETCHES):
        parts[part] = [shift_tp(value, -k) for k, value in zip(ORDER, parts[part])]

    gathered = []
    for part in range(STRETCHES):
        own, taken, keep, give = summed(
            this_core, coords[part], pulled[part], parts[part], chosen[part]
        )
        first = both_cores(this_core, keep, swap_cores(give))
        line = [first] + ordered(lambda k: by_core(first, (k, 0), (0, k)))
        *routed, wide = route_runs(this_core, index, line, each)
        line = routed[:1] + ordered(lambda k: by_core(routed[k], (0, k), (-k, 0)))
        keep, give = finished_runs(this_core, from_row, wide, line, each)
        both = update_and_net(this_core, keep, swap_cores(give), own, chosen[part], taken)
        gathered.append([both] + ordered(lambda k: shift_tp(both, k)))
    near, far = ([value[ORDER.index(k)] for k in (1, 2, 3)] for value in (near, far))
    intervened = intervention(this_core, hidden, gathered, own_block, near, far, length)

    rows = features // (Y * CORES)
    away = gradient_rows(other_core, cotangent, hidden, gathered, length)
    grad = gradient_rows(this_core, cotangent, hidden, gathered, length) + swap_cores(away)
    grad = grad.astype(bf16).reshape(Z * Y, rows, columns)
    grad, intervened = lax.optimization_barrier((grad, intervened))
    groups = [[z * 8 + y * 2 + c for z in range(Z) for y in range(Y)] for c in range(CORES)]
    grad = lax.all_to_all(grad, "runs", 0, 0, axis_index_groups=groups, tiled=True)
    grad = jnp.sum(grad.astype(f32), axis=0)
    home = [
        ((z * 8 + y * 2 + c) * TP + x, (x * 8 + y * 2 + c) * TP + (x - z) % TP)
        for z in range(Z)
        for y in range(Y)
        for c in range(CORES)
        for x in range(TP)
    ]
    return intervened, lax.ppermute(grad, ("runs", "tp"), home)


def solution(mesh):
    def step(*arrays):
        return per_device(*arrays)

    in_specs = (P("runs", "tp"), P("runs", "tp"), P(None, "tp"), P("runs"), P("runs", None))
    out_specs = (P("runs", "tp"), P("runs", "tp"))
    step = jax.shard_map(
        step, mesh=mesh, in_specs=in_specs, out_specs=out_specs, check_vma=False
    )
    return step
```

profile of v0, /device:TPU:6, one launch (start us, length us, event | category | flops | bytes accessed | tf_op | source)
XLA Modules:
  0.0 130.9 jit_solution(9954422143692356948)
XLA Ops:
  0.7 2.4 %dynamic-slice_convert_fusion = (bf16[1024,128]{1,0:T(8,128)(2,1)}, bf16[1024,128]{1,0:T(8,128)(2,1)}, bf16[1024,128]{1,0:T(8,128)(2,1)}) fusion(f32[8192,128]{1,0:T(8,128)} %param.7, s32[]{:T(128)S(6)} %select_n.216, s32[]{:T(128)S(6)} %select_n.212, s32[]{:T(128)S(6)} %select_n.214), kind=kLoop, calls=%fused_computation.2 | loop fusion | bytes 1572876 | tf_op jit(solution)/shard_map/convert_element_type | solution.py:340
  3.5 1.7 %collective-permute-start.5 = (bf16[1024,128]{1,0:T(8,128)(2,1)}, bf16[1024,128]{1,0:T(8,128)(2,1)S(1)}, u32[]{:S(2)}, u32[]{:S(2)}) collective-permute-start(bf16[1024,128]{1,0:T(8,128)(2,1)} %get-tuple-element.88), channel_id=1, source_target_pairs={{0,3},{1,0},{2,1},{3,2},{4,7},{5,4},{6,5},{7,6},{8,11},{9,8},{10,9... | collective-permute-start | bytes 786440 | tf_op jit(solution)/shard_map/ppermute | solution.py:31
  5.1 1.4 %collective-permute-start.6 = (bf16[1024,128]{1,0:T(8,128)(2,1)}, bf16[1024,128]{1,0:T(8,128)(2,1)S(1)}, u32[]{:S(2)}, u32[]{:S(2)}) collective-permute-start(bf16[1024,128]{1,0:T(8,128)(2,1)} %get-tuple-element.86), channel_id=1, source_target_pairs={{0,2},{1,3},{2,0},{3,1},{4,6},{5,7},{6,4},{7,5},{8,10},{9,11},{10,... | collective-permute-start | bytes 786440 | tf_op jit(solution)/shard_map/ppermute | solution.py:31
  6.5 1.3 constant_dynamic-slice_fusion.own_ref
  7.9 1.6 %copy-done.1 = bf16[512,2048]{1,0:T(8,128)(2,1)S(1)} copy-done((bf16[512,2048]{1,0:T(8,128)(2,1)S(1)}, bf16[512,2048]{1,0:T(8,128)(2,1)}, u32[]{:S(2)}) %copy-start.1) | copy-done | bytes 2097176
  9.4 1.2 shard_map.68
  12.7 0.7 copy-done.10
  14.0 4.2 %collective-permute-done.6.refs_2_.refs_9_ = bf16[1024,128]{1,0:T(8,128)(2,1)S(1)} collective-permute-done((bf16[1024,128]{1,0:T(8,128)(2,1)}, bf16[1024,128]{1,0:T(8,128)(2,1)S(1)}, u32[]{:S(2)}, u32[]{:S(2)}) %collective-permute-start.6) | collective-permute-done | bytes 262176 | tf_op jit(solution)/shard_map/ppermute | solution.py:31
  18.7 1.2 collective-permute-done.9.refs_5_.refs_12_
  19.9 1.6 %copy-done.2 = bf16[512,2048]{1,0:T(8,128)(2,1)S(1)} copy-done((bf16[512,2048]{1,0:T(8,128)(2,1)S(1)}, bf16[512,2048]{1,0:T(8,128)(2,1)}, u32[]{:S(2)}) %copy-start.2) | copy-done | bytes 2097176
  21.5 3.5 %shard_map.70 = (bf16[512,128]{1,0:T(8,128)(2,1)S(1)}, bf16[512,128]{1,0:T(8,128)(2,1)S(1)}, bf16[512,128]{1,0:T(8,128)(2,1)S(1)}, bf16[512,128]{1,0:T(8,128)(2,...) custom-call(s32[1]{0:T(128)} %bitcast.core_ref, bf16[512,2048]{1,0:T(8,128)(2,1)S(1)} %copy-done, ...), custom_call_target="tpu_custom_call" | custom-call | flops 1610612736 | tf_op jit(solution)/shard_map/pallas_call | solution.py:68
  25.2 3.7 %collective-permute-start.1 = (s32[8]{0:T(128)S(1)}, s32[8]{0:T(128)S(1)}, u32[]{:S(2)}, u32[]{:S(2)}) collective-permute-start(s32[8]{0:T(128)S(1)} %get-tuple-element.79), channel_id=1, source_target_pairs={{0,24},{4,28},{8,0},{12,4},{16,8},{20,12},{24,16},{28,20},{32,56},... | collective-permute-start | bytes 104 | tf_op jit(solution)/shard_map/ppermute | solution.py:35
  28.8 3.2 %collective-permute-start.25 = (bf16[512,128]{1,0:T(8,128)(2,1)S(1)}, bf16[512,128]{1,0:T(8,128)(2,1)S(1)}, u32[]{:S(2)}, u32[]{:S(2)}) collective-permute-start(bf16[512,128]{1,0:T(8,128)(2,1)S(1)} %get-tuple-element.60), channel_id=1, source_target_pairs={{0,1},{1,2},{2,3},{3,0},{4,5},{5,6},{6,7},{7,4},{8,9},{9,10},{10,1... | collective-permute-start | bytes 393224 | tf_op jit(solution)/shard_map/ppermute | solution.py:31
  32.9 2.6 %collective-permute-start.11 = (bf16[512,128]{1,0:T(8,128)(2,1)S(1)}, bf16[512,128]{1,0:T(8,128)(2,1)S(1)}, u32[]{:S(2)}, u32[]{:S(2)}) collective-permute-start(bf16[512,128]{1,0:T(8,128)(2,1)S(1)} %get-tuple-element.44), channel_id=1, source_target_pairs={{0,1},{1,2},{2,3},{3,0},{4,5},{5,6},{6,7},{7,4},{8,9},{9,10},{10,1... | collective-permute-start | bytes 393224 | tf_op jit(solution)/shard_map/ppermute | solution.py:31
  35.5 2.1 %collective-permute-start.12 = (bf16[512,128]{1,0:T(8,128)(2,1)S(1)}, bf16[512,128]{1,0:T(8,128)(2,1)S(1)}, u32[]{:S(2)}, u32[]{:S(2)}) collective-permute-start(bf16[512,128]{1,0:T(8,128)(2,1)S(1)} %get-tuple-element.45), channel_id=1, source_target_pairs={{0,2},{1,3},{2,0},{3,1},{4,6},{5,7},{6,4},{7,5},{8,10},{9,11},{10,... | collective-permute-start | bytes 393224 | tf_op jit(solution)/shard_map/ppermute | solution.py:31
  38.9 1.1 collective-permute-done.26.refs_2_
  40.1 1.9 %collective-permute-done.10.refs_0_ = bf16[512,128]{1,0:T(8,128)(2,1)S(1)} collective-permute-done((bf16[512,128]{1,0:T(8,128)(2,1)S(1)}, bf16[512,128]{1,0:T(8,128)(2,1)S(1)}, u32[]{:S(2)}, u32[]{:S(2)}) %collective-permute-start.10) | collective-permute-done | bytes 131104 | tf_op jit(solution)/shard_map/ppermute | solution.py:31
  42.1 0.9 collective-permute-done.11.refs_1_
  43.0 0.9 collective-permute-done.12.refs_2_
  44.2 2.0 %collective-permute-start.28 = (bf16[512,128]{1,0:T(8,128)(2,1)S(1)}, bf16[512,128]{1,0:T(8,128)(2,1)S(1)}, u32[]{:S(2)}, u32[]{:S(2)}) collective-permute-start(bf16[512,128]{1,0:T(8,128)(2,1)S(1)} %shard_map.77.refs_0_), channel_id=1, source_target_pairs={{0,32},{8,40},{16,48},{24,56},{32,64},{40,72},{48,80},{56,88},{64,... | collective-permute-start | bytes 393224 | tf_op jit(solution)/shard_map/ppermute | solution.py:40
  46.1 3.6 %collective-permute-start.29 = (bf16[512,128]{1,0:T(8,128)(2,1)S(1)}, bf16[512,128]{1,0:T(8,128)(2,1)S(1)}, u32[]{:S(2)}, u32[]{:S(2)}) collective-permute-start(bf16[512,128]{1,0:T(8,128)(2,1)S(1)} %shard_map.77.refs_0_), channel_id=1, source_target_pairs={{0,64},{8,72},{16,80},{24,88},{32,96},{40,104},{48,112},{56,120},{... | collective-permute-start | bytes 393224 | tf_op jit(solution)/shard_map/ppermute | solution.py:40
  49.7 1.0 collective-permute-start.30
  50.8 1.1 collective-permute-start.14
  52.4 2.2 %collective-permute-start.16 = (bf16[512,128]{1,0:T(8,128)(2,1)S(1)}, bf16[512,128]{1,0:T(8,128)(2,1)S(1)}, u32[]{:S(2)}, u32[]{:S(2)}) collective-permute-start(bf16[512,128]{1,0:T(8,128)(2,1)S(1)} %shard_map.72.refs_0_), channel_id=1, source_target_pairs={{0,96},{8,104},{16,112},{24,120},{32,0},{40,8},{48,16},{56,24},{64... | collective-permute-start | bytes 393224 | tf_op jit(solution)/shard_map/ppermute | solution.py:40
  55.4 2.2 %collective-permute-start.32 = (bf16[512,128]{1,0:T(8,128)(2,1)S(1)}, bf16[512,128]{1,0:T(8,128)(2,1)S(1)}, u32[]{:S(2)}, u32[]{:S(2)}) collective-permute-start(bf16[512,128]{1,0:T(8,128)(2,1)S(1)} %get-tuple-element.67), channel_id=1, source_target_pairs={{0,16},{8,24},{16,0},{24,8},{32,48},{40,56},{48,32},{56,40},{64,80... | collective-permute-start | bytes 393224 | tf_op jit(solution)/shard_map/ppermute | solution.py:40
  57.6 1.1 collective-permute-start.33
  58.7 2.6 %collective-permute-done.16.refs_3_ = bf16[512,128]{1,0:T(8,128)(2,1)S(1)} collective-permute-done((bf16[512,128]{1,0:T(8,128)(2,1)S(1)}, bf16[512,128]{1,0:T(8,128)(2,1)S(1)}, u32[]{:S(2)}, u32[]{:S(2)}) %collective-permute-start.16) | collective-permute-done | bytes 131104 | tf_op jit(solution)/shard_map/ppermute | solution.py:40
  62.0 2.5 %collective-permute-start.18 = (bf16[512,128]{1,0:T(8,128)(2,1)S(1)}, bf16[512,128]{1,0:T(8,128)(2,1)S(1)}, u32[]{:S(2)}, u32[]{:S(2)}) collective-permute-start(bf16[512,128]{1,0:T(8,128)(2,1)S(1)} %get-tuple-element.51), channel_id=1, source_target_pairs={{0,16},{8,24},{16,0},{24,8},{32,48},{40,56},{48,32},{56,40},{64,80... | collective-permute-start | bytes 393224 | tf_op jit(solution)/shard_map/ppermute | solution.py:40
  64.5 0.9 collective-permute-start.19
  66.1 3.4 %collective-permute-done.17.refs_1_ = bf16[512,128]{1,0:T(8,128)(2,1)S(1)} collective-permute-done((bf16[512,128]{1,0:T(8,128)(2,1)S(1)}, bf16[512,128]{1,0:T(8,128)(2,1)S(1)}, u32[]{:S(2)}, u32[]{:S(2)}) %collective-permute-start.17) | collective-permute-done | bytes 131104 | tf_op jit(solution)/shard_map/ppermute | solution.py:40
  69.6 0.9 collective-permute-done.19.refs_3_
  71.3 3.2 %collective-permute-start.35 = (bf16[512,128]{1,0:T(8,128)(2,1)S(1)}, bf16[512,128]{1,0:T(8,128)(2,1)S(1)}, u32[]{:S(2)}, u32[]{:S(2)}) collective-permute-start(bf16[512,128]{1,0:T(8,128)(2,1)S(1)} %shard_map.80.refs_4_), channel_id=1, source_target_pairs={{0,1},{1,2},{2,3},{3,0},{4,5},{5,6},{6,7},{7,4},{8,9},{9,10},{10,1... | collective-permute-start | bytes 393224 | tf_op jit(solution)/shard_map/ppermute | solution.py:31
  74.4 0.9 collective-permute-start.37
  75.4 2.4 %collective-permute-start.21 = (bf16[512,128]{1,0:T(8,128)(2,1)S(1)}, bf16[512,128]{1,0:T(8,128)(2,1)S(1)}, u32[]{:S(2)}, u32[]{:S(2)}) collective-permute-start(bf16[512,128]{1,0:T(8,128)(2,1)S(1)} %shard_map.75.refs_0_), channel_id=1, source_target_pairs={{0,1},{1,2},{2,3},{3,0},{4,5},{5,6},{6,7},{7,4},{8,9},{9,10},{10,1... | collective-permute-start | bytes 393224 | tf_op jit(solution)/shard_map/ppermute | solution.py:31
  77.8 2.3 %collective-permute-start.22 = (bf16[512,128]{1,0:T(8,128)(2,1)S(1)}, bf16[512,128]{1,0:T(8,128)(2,1)S(1)}, u32[]{:S(2)}, u32[]{:S(2)}) collective-permute-start(bf16[512,128]{1,0:T(8,128)(2,1)S(1)} %shard_map.75.refs_0_), channel_id=1, source_target_pairs={{0,2},{1,3},{2,0},{3,1},{4,6},{5,7},{6,4},{7,5},{8,10},{9,11},{10,... | collective-permute-start | bytes 393224 | tf_op jit(solution)/shard_map/ppermute | solution.py:31
  80.1 1.0 collective-permute-done.35.refs_5_
  81.1 1.2 collective-permute-done.36.refs_6_
  82.3 2.1 %collective-permute-done.37.refs_7_ = bf16[512,128]{1,0:T(8,128)(2,1)S(1)} collective-permute-done((bf16[512,128]{1,0:T(8,128)(2,1)S(1)}, bf16[512,128]{1,0:T(8,128)(2,1)S(1)}, u32[]{:S(2)}, u32[]{:S(2)}) %collective-permute-start.37) | collective-permute-done | bytes 131104 | tf_op jit(solution)/shard_map/ppermute | solution.py:31
  84.5 1.8 %collective-permute-done.21.refs_1_ = bf16[512,128]{1,0:T(8,128)(2,1)S(1)} collective-permute-done((bf16[512,128]{1,0:T(8,128)(2,1)S(1)}, bf16[512,128]{1,0:T(8,128)(2,1)S(1)}, u32[]{:S(2)}, u32[]{:S(2)}) %collective-permute-start.21) | collective-permute-done | bytes 131104 | tf_op jit(solution)/shard_map/ppermute | solution.py:31
  86.2 1.8 %collective-permute-done.22.refs_2_ = bf16[512,128]{1,0:T(8,128)(2,1)S(1)} collective-permute-done((bf16[512,128]{1,0:T(8,128)(2,1)S(1)}, bf16[512,128]{1,0:T(8,128)(2,1)S(1)}, u32[]{:S(2)}, u32[]{:S(2)}) %collective-permute-start.22) | collective-permute-done | bytes 131104 | tf_op jit(solution)/shard_map/ppermute | solution.py:31
  88.0 1.8 %collective-permute-done.23.refs_3_ = bf16[512,128]{1,0:T(8,128)(2,1)S(1)} collective-permute-done((bf16[512,128]{1,0:T(8,128)(2,1)S(1)}, bf16[512,128]{1,0:T(8,128)(2,1)S(1)}, u32[]{:S(2)}, u32[]{:S(2)}) %collective-permute-start.23) | collective-permute-done | bytes 131104 | tf_op jit(solution)/shard_map/ppermute | solution.py:31
  89.8 1.3 shard_map.82
  91.2 1.3 shard_map.81
  92.5 3.7 %shard_map.83 = bf16[512,2048]{1,0:T(8,128)(2,1)} custom-call(s32[1]{0:T(128)} %bitcast.core_ref, bf16[512,2048]{1,0:T(8,128)(2,1)S(1)} %copy-done, bf16[2048,128]{1,0:T(8,128)(2,1)S(1)} %get-tuple-element.73.own_ref, bf16[512,128]{1,0:T(8,128)(2,1)S(1)} %shard_map.75.refs_0_, bf16[512,128]{1,0:T(8,128)(2,1)S(1)} %collective-permute-done.21.refs_1_, ...), custom_call_target="tpu_custom_call" | custom-call | flops 1073741824 | tf_op jit(solution)/shard_map/pallas_call | solution.py:68
  96.5 24.7 %all_to_all.5 = bf16[16,256,128]{2,1,0:T(8,128)(2,1)S(1)} all-to-all(bf16[16,256,128]{2,1,0:T(8,128)(2,1)S(1)} %bitcast.2), channel_id=1, replica_groups={{0,8,16,24,32,40,48,56,64,72,80,88,96,104,112,120},{4,12,20,28,36,44,52..., dimensions={0} | all-to-all | bytes 2097152 | tf_op jit(solution)/shard_map/all_to_all | solution.py:407
  121.3 2.8 %collective-permute-start.39 = (f32[256,128]{1,0:T(8,128)S(1)}, f32[256,128]{1,0:T(8,128)S(1)}, u32[]{:S(2)}, u32[]{:S(2)}) collective-permute-start(f32[256,128]{1,0:T(8,128)S(1)} %convert_reduce_fusion), channel_id=1, source_target_pairs={{0,0},{1,33},{2,66},{3,99},{4,4},{5,37},{6,70},{7,103},{8,8},{9,41... | collective-permute-start | bytes 393224 | tf_op jit(solution)/shard_map/ppermute | solution.py:416
  124.1 6.2 %collective-permute-done.39 = f32[256,128]{1,0:T(8,128)S(1)} collective-permute-done((f32[256,128]{1,0:T(8,128)S(1)}, f32[256,128]{1,0:T(8,128)S(1)}, u32[]{:S(2)}, u32[]{:S(2)}) %collective-permute-start.39) | collective-permute-done | bytes 131104 | tf_op jit(solution)/shard_map/ppermute | solution.py:416
  130.3 0.7 copy.8
  (96 shorter events, 10.1 us)
Async XLA Ops:
  0.6 7.2 %copy-start = (bf16[512,2048]{1,0:T(8,128)(2,1)S(1)}, bf16[512,2048]{1,0:T(8,128)(2,1)}, u32[]{:S(2)}) copy-start(bf16[512,2048]{1,0:T(8,128)(2,1)} %hidden_ref.9) | copy-start | bytes 6291460
  3.1 10.2 %collective-permute-start.4 = (bf16[1024,128]{1,0:T(8,128)(2,1)}, bf16[1024,128]{1,0:T(8,128)(2,1)S(1)}, u32[]{:S(2)}, u32[]{:S(2)}) collective-permute-start(bf16[1024,128]{1,0:T(8,128)(2,1)} %get-tuple-element.87), channel_id=1, source_target_pairs={{0,1},{1,2},{2,3},{3,0},{4,5},{5,6},{6,7},{7,4},{8,9},{9,10},{10,1... | collective-permute-start | bytes 786440 | tf_op jit(solution)/shard_map/ppermute | solution.py:31
  3.5 10.5 %collective-permute-start.5 = (bf16[1024,128]{1,0:T(8,128)(2,1)}, bf16[1024,128]{1,0:T(8,128)(2,1)S(1)}, u32[]{:S(2)}, u32[]{:S(2)}) collective-permute-start(bf16[1024,128]{1,0:T(8,128)(2,1)} %get-tuple-element.88), channel_id=1, source_target_pairs={{0,3},{1,0},{2,1},{3,2},{4,7},{5,4},{6,5},{7,6},{8,11},{9,8},{10,9... | collective-permute-start | bytes 786440 | tf_op jit(solution)/shard_map/ppermute | solution.py:31
  5.1 13.1 %collective-permute-start.6 = (bf16[1024,128]{1,0:T(8,128)(2,1)}, bf16[1024,128]{1,0:T(8,128)(2,1)S(1)}, u32[]{:S(2)}, u32[]{:S(2)}) collective-permute-start(bf16[1024,128]{1,0:T(8,128)(2,1)} %get-tuple-element.86), channel_id=1, source_target_pairs={{0,2},{1,3},{2,0},{3,1},{4,6},{5,7},{6,4},{7,5},{8,10},{9,11},{10,... | collective-permute-start | bytes 786440 | tf_op jit(solution)/shard_map/ppermute | solution.py:31
  9.4 3.9 %copy-start.13 = (s32[4]{0:T(128)S(1)}, s32[4]{0:T(128)}, u32[]{:S(2)}) copy-start(s32[4]{0:T(128)} %param.8) | copy-start | bytes 52
  9.4 8.8 %copy-start.12 = (s32[4,128]{1,0:T(4,128)S(1)}, s32[4,128]{1,0:T(4,128)}, u32[]{:S(2)}) copy-start(s32[4,128]{1,0:T(4,128)} %param.9) | copy-start | bytes 6148
  13.3 11.7 %collective-permute-start = (s32[4]{0:T(128)S(1)}, s32[4]{0:T(128)S(1)}, u32[]{:S(2)}, u32[]{:S(2)}) collective-permute-start(s32[4]{0:T(128)S(1)} %copy-done.13), channel_id=1, source_target_pairs={{0,4},{4,0},{8,12},{12,8},{16,20},{20,16},{24,28},{28,24},{32,36},... | collective-permute-start | bytes 56 | tf_op jit(solution)/shard_map/ppermute | solution.py:44
  13.3 5.3 %collective-permute-start.7 = (bf16[1024,128]{1,0:T(8,128)(2,1)S(1)}, bf16[1024,128]{1,0:T(8,128)(2,1)}, u32[]{:S(2)}, u32[]{:S(2)}) collective-permute-start(bf16[1024,128]{1,0:T(8,128)(2,1)S(1)} %collective-permute-done.4.refs_0_.refs_8_), channel_id=1, source_target_pairs={{0,4},{4,0},{8,12},{12,8},{16,20},{20,16},{24,28},{28,24},{32,36},... | collective-permute-start | bytes 786440 | tf_op jit(solution)/shard_map/ppermute | solution.py:44
  14.0 4.7 %collective-permute-start.8 = (bf16[1024,128]{1,0:T(8,128)(2,1)S(1)}, bf16[1024,128]{1,0:T(8,128)(2,1)}, u32[]{:S(2)}, u32[]{:S(2)}) collective-permute-start(bf16[1024,128]{1,0:T(8,128)(2,1)S(1)} %collective-permute-done.5.refs_1_.refs_10_), channel_id=1, source_target_pairs={{0,4},{4,0},{8,12},{12,8},{16,20},{20,16},{24,28},{28,24},{32,36},... | collective-permute-start | bytes 786440 | tf_op jit(solution)/shard_map/ppermute | solution.py:44
  18.2 1.7 %collective-permute-start.9 = (bf16[1024,128]{1,0:T(8,128)(2,1)S(1)}, bf16[1024,128]{1,0:T(8,128)(2,1)}, u32[]{:S(2)}, u32[]{:S(2)}) collective-permute-start(bf16[1024,128]{1,0:T(8,128)(2,1)S(1)} %collective-permute-done.6.refs_2_.refs_9_), channel_id=1, source_target_pairs={{0,4},{4,0},{8,12},{12,8},{16,20},{20,16},{24,28},{28,24},{32,36},... | collective-permute-start | bytes 786440 | tf_op jit(solution)/shard_map/ppermute | solution.py:44
  21.5 18.6 %copy-start.9 = (f32[256,128]{1,0:T(8,128)S(1)}, f32[256,128]{1,0:T(8,128)}, u32[]{:S(2)}) copy-start(f32[256,128]{1,0:T(8,128)} %copy-done.8) | copy-start | bytes 393220
  21.5 18.6 %copy-start.11 = (f32[256,128]{1,0:T(8,128)S(1)}, f32[256,128]{1,0:T(8,128)}, u32[]{:S(2)}) copy-start(f32[256,128]{1,0:T(8,128)} %copy-done.10) | copy-start | bytes 393220
  21.5 22.4 %copy-start.5 = (f32[256,128]{1,0:T(8,128)S(1)}, f32[256,128]{1,0:T(8,128)}, u32[]{:S(2)}) copy-start(f32[256,128]{1,0:T(8,128)} %copy-done.4) | copy-start | bytes 393220
  21.5 22.4 %copy-start.7 = (f32[256,128]{1,0:T(8,128)S(1)}, f32[256,128]{1,0:T(8,128)}, u32[]{:S(2)}) copy-start(f32[256,128]{1,0:T(8,128)} %copy-done.6) | copy-start | bytes 393220
  25.0 10.6 %collective-permute-start.24 = (bf16[512,128]{1,0:T(8,128)(2,1)S(1)}, bf16[512,128]{1,0:T(8,128)(2,1)S(1)}, u32[]{:S(2)}, u32[]{:S(2)}) collective-permute-start(bf16[512,128]{1,0:T(8,128)(2,1)S(1)} %get-tuple-element.59), channel_id=1, source_target_pairs={{0,3},{1,0},{2,1},{3,2},{4,7},{5,4},{6,5},{7,6},{8,11},{9,8},{10,9... | collective-permute-start | bytes 393224 | tf_op jit(solution)/shard_map/ppermute | solution.py:31
  25.2 7.7 %collective-permute-start.1 = (s32[8]{0:T(128)S(1)}, s32[8]{0:T(128)S(1)}, u32[]{:S(2)}, u32[]{:S(2)}) collective-permute-start(s32[8]{0:T(128)S(1)} %get-tuple-element.79), channel_id=1, source_target_pairs={{0,24},{4,28},{8,0},{12,4},{16,8},{20,12},{24,16},{28,20},{32,56},... | collective-permute-start | bytes 104 | tf_op jit(solution)/shard_map/ppermute | solution.py:35
  28.8 9.4 %collective-permute-start.25 = (bf16[512,128]{1,0:T(8,128)(2,1)S(1)}, bf16[512,128]{1,0:T(8,128)(2,1)S(1)}, u32[]{:S(2)}, u32[]{:S(2)}) collective-permute-start(bf16[512,128]{1,0:T(8,128)(2,1)S(1)} %get-tuple-element.60), channel_id=1, source_target_pairs={{0,1},{1,2},{2,3},{3,0},{4,5},{5,6},{6,7},{7,4},{8,9},{9,10},{10,1... | collective-permute-start | bytes 393224 | tf_op jit(solution)/shard_map/ppermute | solution.py:31
  32.0 7.9 %collective-permute-start.26 = (bf16[512,128]{1,0:T(8,128)(2,1)S(1)}, bf16[512,128]{1,0:T(8,128)(2,1)S(1)}, u32[]{:S(2)}, u32[]{:S(2)}) collective-permute-start(bf16[512,128]{1,0:T(8,128)(2,1)S(1)} %get-tuple-element.61), channel_id=1, source_target_pairs={{0,2},{1,3},{2,0},{3,1},{4,6},{5,7},{6,4},{7,5},{8,10},{9,11},{10,... | collective-permute-start | bytes 393224 | tf_op jit(solution)/shard_map/ppermute | solution.py:31
  32.3 9.8 %collective-permute-start.10 = (bf16[512,128]{1,0:T(8,128)(2,1)S(1)}, bf16[512,128]{1,0:T(8,128)(2,1)S(1)}, u32[]{:S(2)}, u32[]{:S(2)}) collective-permute-start(bf16[512,128]{1,0:T(8,128)(2,1)S(1)} %get-tuple-element.43), channel_id=1, source_target_pairs={{0,3},{1,0},{2,1},{3,2},{4,7},{5,4},{6,5},{7,6},{8,11},{9,8},{10,9... | collective-permute-start | bytes 393224 | tf_op jit(solution)/shard_map/ppermute | solution.py:31
  32.9 10.1 %collective-permute-start.11 = (bf16[512,128]{1,0:T(8,128)(2,1)S(1)}, bf16[512,128]{1,0:T(8,128)(2,1)S(1)}, u32[]{:S(2)}, u32[]{:S(2)}) collective-permute-start(bf16[512,128]{1,0:T(8,128)(2,1)S(1)} %get-tuple-element.44), channel_id=1, source_target_pairs={{0,1},{1,2},{2,3},{3,0},{4,5},{5,6},{6,7},{7,4},{8,9},{9,10},{10,1... | collective-permute-start | bytes 393224 | tf_op jit(solution)/shard_map/ppermute | solution.py:31
  35.5 8.4 %collective-permute-start.12 = (bf16[512,128]{1,0:T(8,128)(2,1)S(1)}, bf16[512,128]{1,0:T(8,128)(2,1)S(1)}, u32[]{:S(2)}, u32[]{:S(2)}) collective-permute-start(bf16[512,128]{1,0:T(8,128)(2,1)S(1)} %get-tuple-element.45), channel_id=1, source_target_pairs={{0,2},{1,3},{2,0},{3,1},{4,6},{5,7},{6,4},{7,5},{8,10},{9,11},{10,... | collective-permute-start | bytes 393224 | tf_op jit(solution)/shard_map/ppermute | solution.py:31
  38.2 5.9 %collective-permute-start.2 = (s32[8]{0:T(128)S(1)}, s32[8]{0:T(128)S(1)}, u32[]{:S(2)}, u32[]{:S(2)}) collective-permute-start(s32[8]{0:T(128)S(1)} %get-tuple-element.79), channel_id=1, source_target_pairs={{0,16},{4,20},{8,24},{12,28},{16,0},{20,4},{24,8},{28,12},{32,48},... | collective-permute-start | bytes 104 | tf_op jit(solution)/shard_map/ppermute | solution.py:35
  39.9 11.9 %collective-permute-start.3 = (s32[8]{0:T(128)S(1)}, s32[8]{0:T(128)S(1)}, u32[]{:S(2)}, u32[]{:S(2)}) collective-permute-start(s32[8]{0:T(128)S(1)} %get-tuple-element.79), channel_id=1, source_target_pairs={{0,8},{4,12},{8,16},{12,20},{16,24},{20,28},{24,0},{28,4},{32,40},... | collective-permute-start | bytes 104 | tf_op jit(solution)/shard_map/ppermute | solution.py:35
  42.1 2.1 %collective-permute-start.27 = (bf16[256,128]{1,0:T(8,128)(2,1)S(1)}, bf16[256,128]{1,0:T(8,128)(2,1)S(1)}, u32[]{:S(2)}, u32[]{:S(2)}) collective-permute-start(bf16[256,128]{1,0:T(8,128)(2,1)S(1)} %get-tuple-element.63), channel_id=1, source_target_pairs={{0,4},{4,0},{8,12},{12,8},{16,20},{20,16},{24,28},{28,24},{32,36},... | collective-permute-start | bytes 196616 | tf_op jit(solution)/shard_map/ppermute | solution.py:44
  44.0 6.7 %collective-permute-start.13 = (bf16[256,128]{1,0:T(8,128)(2,1)S(1)}, bf16[256,128]{1,0:T(8,128)(2,1)S(1)}, u32[]{:S(2)}, u32[]{:S(2)}) collective-permute-start(bf16[256,128]{1,0:T(8,128)(2,1)S(1)} %get-tuple-element.47), channel_id=1, source_target_pairs={{0,4},{4,0},{8,12},{12,8},{16,20},{20,16},{24,28},{28,24},{32,36},... | collective-permute-start | bytes 196616 | tf_op jit(solution)/shard_map/ppermute | solution.py:44
  44.2 8.3 %collective-permute-start.28 = (bf16[512,128]{1,0:T(8,128)(2,1)S(1)}, bf16[512,128]{1,0:T(8,128)(2,1)S(1)}, u32[]{:S(2)}, u32[]{:S(2)}) collective-permute-start(bf16[512,128]{1,0:T(8,128)(2,1)S(1)} %shard_map.77.refs_0_), channel_id=1, source_target_pairs={{0,32},{8,40},{16,48},{24,56},{32,64},{40,72},{48,80},{56,88},{64,... | collective-permute-start | bytes 393224 | tf_op jit(solution)/shard_map/ppermute | solution.py:40
  46.1 8.5 %collective-permute-start.29 = (bf16[512,128]{1,0:T(8,128)(2,1)S(1)}, bf16[512,128]{1,0:T(8,128)(2,1)S(1)}, u32[]{:S(2)}, u32[]{:S(2)}) collective-permute-start(bf16[512,128]{1,0:T(8,128)(2,1)S(1)} %shard_map.77.refs_0_), channel_id=1, source_target_pairs={{0,64},{8,72},{16,80},{24,88},{32,96},{40,104},{48,112},{56,120},{... | collective-permute-start | bytes 393224 | tf_op jit(solution)/shard_map/ppermute | solution.py:40
  49.7 5.0 %collective-permute-start.30 = (bf16[512,128]{1,0:T(8,128)(2,1)S(1)}, bf16[512,128]{1,0:T(8,128)(2,1)S(1)}, u32[]{:S(2)}, u32[]{:S(2)}) collective-permute-start(bf16[512,128]{1,0:T(8,128)(2,1)S(1)} %shard_map.77.refs_0_), channel_id=1, source_target_pairs={{0,96},{8,104},{16,112},{24,120},{32,0},{40,8},{48,16},{56,24},{64... | collective-permute-start | bytes 393224 | tf_op jit(solution)/shard_map/ppermute | solution.py:40
  50.8 6.9 %collective-permute-start.14 = (bf16[512,128]{1,0:T(8,128)(2,1)S(1)}, bf16[512,128]{1,0:T(8,128)(2,1)S(1)}, u32[]{:S(2)}, u32[]{:S(2)}) collective-permute-start(bf16[512,128]{1,0:T(8,128)(2,1)S(1)} %shard_map.72.refs_0_), channel_id=1, source_target_pairs={{0,32},{8,40},{16,48},{24,56},{32,64},{40,72},{48,80},{56,88},{64,... | collective-permute-start | bytes 393224 | tf_op jit(solution)/shard_map/ppermute | solution.py:40
  51.9 37.9 %copy-start.3 = (bf16[512,2048]{1,0:T(8,128)(2,1)S(1)}, bf16[512,2048]{1,0:T(8,128)(2,1)}, u32[]{:S(2)}) copy-start(bf16[512,2048]{1,0:T(8,128)(2,1)} %cotangent_ref.7) | copy-start | bytes 6291460
  51.9 6.7 %collective-permute-start.15 = (bf16[512,128]{1,0:T(8,128)(2,1)S(1)}, bf16[512,128]{1,0:T(8,128)(2,1)S(1)}, u32[]{:S(2)}, u32[]{:S(2)}) collective-permute-start(bf16[512,128]{1,0:T(8,128)(2,1)S(1)} %shard_map.72.refs_0_), channel_id=1, source_target_pairs={{0,64},{8,72},{16,80},{24,88},{32,96},{40,104},{48,112},{56,120},{... | collective-permute-start | bytes 393224 | tf_op jit(solution)/shard_map/ppermute | solution.py:40
  52.4 8.8 %collective-permute-start.16 = (bf16[512,128]{1,0:T(8,128)(2,1)S(1)}, bf16[512,128]{1,0:T(8,128)(2,1)S(1)}, u32[]{:S(2)}, u32[]{:S(2)}) collective-permute-start(bf16[512,128]{1,0:T(8,128)(2,1)S(1)} %shard_map.72.refs_0_), channel_id=1, source_target_pairs={{0,96},{8,104},{16,112},{24,120},{32,0},{40,8},{48,16},{56,24},{64... | collective-permute-start | bytes 393224 | tf_op jit(solution)/shard_map/ppermute | solution.py:40
  55.3 9.2 %collective-permute-start.31 = (bf16[512,128]{1,0:T(8,128)(2,1)S(1)}, bf16[512,128]{1,0:T(8,128)(2,1)S(1)}, u32[]{:S(2)}, u32[]{:S(2)}) collective-permute-start(bf16[512,128]{1,0:T(8,128)(2,1)S(1)} %get-tuple-element.66), channel_id=1, source_target_pairs={{0,8},{8,16},{16,24},{24,0},{32,40},{40,48},{48,56},{56,32},{64,72... | collective-permute-start | bytes 393224 | tf_op jit(solution)/shard_map/ppermute | solution.py:40
  55.4 10.0 %collective-permute-start.32 = (bf16[512,128]{1,0:T(8,128)(2,1)S(1)}, bf16[512,128]{1,0:T(8,128)(2,1)S(1)}, u32[]{:S(2)}, u32[]{:S(2)}) collective-permute-start(bf16[512,128]{1,0:T(8,128)(2,1)S(1)} %get-tuple-element.67), channel_id=1, source_target_pairs={{0,16},{8,24},{16,0},{24,8},{32,48},{40,56},{48,32},{56,40},{64,80... | collective-permute-start | bytes 393224 | tf_op jit(solution)/shard_map/ppermute | solution.py:40
  57.6 7.8 %collective-permute-start.33 = (bf16[512,128]{1,0:T(8,128)(2,1)S(1)}, bf16[512,128]{1,0:T(8,128)(2,1)S(1)}, u32[]{:S(2)}, u32[]{:S(2)}) collective-permute-start(bf16[512,128]{1,0:T(8,128)(2,1)S(1)} %get-tuple-element.68), channel_id=1, source_target_pairs={{0,24},{8,0},{16,8},{24,16},{32,56},{40,32},{48,40},{56,48},{64,88... | collective-permute-start | bytes 393224 | tf_op jit(solution)/shard_map/ppermute | solution.py:40
  61.9 7.7 %collective-permute-start.17 = (bf16[512,128]{1,0:T(8,128)(2,1)S(1)}, bf16[512,128]{1,0:T(8,128)(2,1)S(1)}, u32[]{:S(2)}, u32[]{:S(2)}) collective-permute-start(bf16[512,128]{1,0:T(8,128)(2,1)S(1)} %get-tuple-element.50), channel_id=1, source_target_pairs={{0,8},{8,16},{16,24},{24,0},{32,40},{40,48},{48,56},{56,32},{64,72... | collective-permute-start | bytes 393224 | tf_op jit(solution)/shard_map/ppermute | solution.py:40
  62.0 7.6 %collective-permute-start.18 = (bf16[512,128]{1,0:T(8,128)(2,1)S(1)}, bf16[512,128]{1,0:T(8,128)(2,1)S(1)}, u32[]{:S(2)}, u32[]{:S(2)}) collective-permute-start(bf16[512,128]{1,0:T(8,128)(2,1)S(1)} %get-tuple-element.51), channel_id=1, source_target_pairs={{0,16},{8,24},{16,0},{24,8},{32,48},{40,56},{48,32},{56,40},{64,80... | collective-permute-start | bytes 393224 | tf_op jit(solution)/shard_map/ppermute | solution.py:40
  64.5 5.9 %collective-permute-start.19 = (bf16[512,128]{1,0:T(8,128)(2,1)S(1)}, bf16[512,128]{1,0:T(8,128)(2,1)S(1)}, u32[]{:S(2)}, u32[]{:S(2)}) collective-permute-start(bf16[512,128]{1,0:T(8,128)(2,1)S(1)} %get-tuple-element.52), channel_id=1, source_target_pairs={{0,24},{8,0},{16,8},{24,16},{32,56},{40,32},{48,40},{56,48},{64,88... | collective-permute-start | bytes 393224 | tf_op jit(solution)/shard_map/ppermute | solution.py:40
  66.0 5.2 %collective-permute-start.34 = (f32[256,128]{1,0:T(8,128)S(1)}, f32[256,128]{1,0:T(8,128)S(1)}, u32[]{:S(2)}, u32[]{:S(2)}) collective-permute-start(f32[256,128]{1,0:T(8,128)S(1)} %get-tuple-element.70), channel_id=1, source_target_pairs={{0,4},{4,0},{8,12},{12,8},{16,20},{20,16},{24,28},{28,24},{32,36},... | collective-permute-start | bytes 393224 | tf_op jit(solution)/shard_map/ppermute | solution.py:44
  71.1 4.3 %collective-permute-start.20 = (f32[256,128]{1,0:T(8,128)S(1)}, f32[256,128]{1,0:T(8,128)S(1)}, u32[]{:S(2)}, u32[]{:S(2)}) collective-permute-start(f32[256,128]{1,0:T(8,128)S(1)} %get-tuple-element.54), channel_id=1, source_target_pairs={{0,4},{4,0},{8,12},{12,8},{16,20},{20,16},{24,28},{28,24},{32,36},... | collective-permute-start | bytes 393224 | tf_op jit(solution)/shard_map/ppermute | solution.py:44
  71.3 9.9 %collective-permute-start.35 = (bf16[512,128]{1,0:T(8,128)(2,1)S(1)}, bf16[512,128]{1,0:T(8,128)(2,1)S(1)}, u32[]{:S(2)}, u32[]{:S(2)}) collective-permute-start(bf16[512,128]{1,0:T(8,128)(2,1)S(1)} %shard_map.80.refs_4_), channel_id=1, source_target_pairs={{0,1},{1,2},{2,3},{3,0},{4,5},{5,6},{6,7},{7,4},{8,9},{9,10},{10,1... | collective-permute-start | bytes 393224 | tf_op jit(solution)/shard_map/ppermute | solution.py:31
  74.4 7.9 %collective-permute-start.36 = (bf16[512,128]{1,0:T(8,128)(2,1)S(1)}, bf16[512,128]{1,0:T(8,128)(2,1)S(1)}, u32[]{:S(2)}, u32[]{:S(2)}) collective-permute-start(bf16[512,128]{1,0:T(8,128)(2,1)S(1)} %shard_map.80.refs_4_), channel_id=1, source_target_pairs={{0,2},{1,3},{2,0},{3,1},{4,6},{5,7},{6,4},{7,5},{8,10},{9,11},{10,... | collective-permute-start | bytes 393224 | tf_op jit(solution)/shard_map/ppermute | solution.py:31
  74.4 10.1 %collective-permute-start.37 = (bf16[512,128]{1,0:T(8,128)(2,1)S(1)}, bf16[512,128]{1,0:T(8,128)(2,1)S(1)}, u32[]{:S(2)}, u32[]{:S(2)}) collective-permute-start(bf16[512,128]{1,0:T(8,128)(2,1)S(1)} %shard_map.80.refs_4_), channel_id=1, source_target_pairs={{0,3},{1,0},{2,1},{3,2},{4,7},{5,4},{6,5},{7,6},{8,11},{9,8},{10,9... | collective-permute-start | bytes 393224 | tf_op jit(solution)/shard_map/ppermute | solution.py:31
  75.4 10.8 %collective-permute-start.21 = (bf16[512,128]{1,0:T(8,128)(2,1)S(1)}, bf16[512,128]{1,0:T(8,128)(2,1)S(1)}, u32[]{:S(2)}, u32[]{:S(2)}) collective-permute-start(bf16[512,128]{1,0:T(8,128)(2,1)S(1)} %shard_map.75.refs_0_), channel_id=1, source_target_pairs={{0,1},{1,2},{2,3},{3,0},{4,5},{5,6},{6,7},{7,4},{8,9},{9,10},{10,1... | collective-permute-start | bytes 393224 | tf_op jit(solution)/shard_map/ppermute | solution.py:31
  77.8 10.2 %collective-permute-start.22 = (bf16[512,128]{1,0:T(8,128)(2,1)S(1)}, bf16[512,128]{1,0:T(8,128)(2,1)S(1)}, u32[]{:S(2)}, u32[]{:S(2)}) collective-permute-start(bf16[512,128]{1,0:T(8,128)(2,1)S(1)} %shard_map.75.refs_0_), channel_id=1, source_target_pairs={{0,2},{1,3},{2,0},{3,1},{4,6},{5,7},{6,4},{7,5},{8,10},{9,11},{10,... | collective-permute-start | bytes 393224 | tf_op jit(solution)/shard_map/ppermute | solution.py:31
  81.1 8.7 %collective-permute-start.23 = (bf16[512,128]{1,0:T(8,128)(2,1)S(1)}, bf16[512,128]{1,0:T(8,128)(2,1)S(1)}, u32[]{:S(2)}, u32[]{:S(2)}) collective-permute-start(bf16[512,128]{1,0:T(8,128)(2,1)S(1)} %shard_map.75.refs_0_), channel_id=1, source_target_pairs={{0,3},{1,0},{2,1},{3,2},{4,7},{5,4},{6,5},{7,6},{8,11},{9,8},{10,9... | collective-permute-start | bytes 393224 | tf_op jit(solution)/shard_map/ppermute | solution.py:31
  91.1 5.1 %collective-permute-start.38 = (f32[4096,128]{1,0:T(8,128)S(1)}, f32[4096,128]{1,0:T(8,128)S(1)}, u32[]{:S(2)}, u32[]{:S(2)}) collective-permute-start(f32[4096,128]{1,0:T(8,128)S(1)} %shard_map.82), channel_id=1, source_target_pairs={{0,4},{4,0},{8,12},{12,8},{16,20},{20,16},{24,28},{28,24},{32,36},... | collective-permute-start | bytes 6291464 | tf_op jit(solution)/shard_map/ppermute | solution.py:44
  121.3 9.0 %collective-permute-start.39 = (f32[256,128]{1,0:T(8,128)S(1)}, f32[256,128]{1,0:T(8,128)S(1)}, u32[]{:S(2)}, u32[]{:S(2)}) collective-permute-start(f32[256,128]{1,0:T(8,128)S(1)} %convert_reduce_fusion), channel_id=1, source_target_pairs={{0,0},{1,33},{2,66},{3,99},{4,4},{5,37},{6,70},{7,103},{8,8},{9,41... | collective-permute-start | bytes 393224 | tf_op jit(solution)/shard_map/ppermute | solution.py:416
  (6 other events, 5.8 us)
where the time goes:
time: 131 us
  starting transfers between devices  46.2 us (35%)
  waiting for transfers between devices  33.9 us (26%)
  blocking collectives  24.7 us (19%)
  Pallas kernels  13.9 us (11%)
  local copies, waits for them, and re-layouts  10.6 us (8%)
    all_to_all x1, blocking collectives, per_device(): lax.all_to_all(grad, 'runs', 0, 0, axis_index_groups=groups, tiled=True)  24.7 us
    ppermute x15, starting transfers between devices, shift_tp(): return lax.ppermute(value, 'tp', along_tp(dx)) if dx % TP else value  21.1 us
    ppermute x15, waiting for transfers between devices, shift_tp(): return lax.ppermute(value, 'tp', along_tp(dx)) if dx % TP else value  19.5 us
    ppermute x12, starting transfers between devices, by_core(): return lax.ppermute(value, 'runs', pairs)  17.2 us
    pallas_call x16, Pallas kernels, kernel(): return call(*scalars, *arrays)  13.9 us
    ppermute x12, waiting for transfers between devices, by_core(): return lax.ppermute(value, 'runs', pairs)  6.94 us
    unnamed x29, local copies, waits for them, and re-layouts  6.47 us
    ppermute x1, waiting for transfers between devices, per_device(): return (intervened, lax.ppermute(grad, ('runs', 'tp'), home))  6.2 us
  transfers between devices with their start and end apart: 40, of which 18 were waited for; matrix products, arithmetic and copies ran while one was open for 2% of the time, Pallas kernels for 10%

commit v1 on v0

--- a/solution.py
+++ b/solution.py
@@ -162,11 +162,15 @@
     )
 
 
-def copied(value):
-    def body(value_ref, out):
-        out[...] = value_ref[...]
-
-    return kernel(body, [(value.shape, value.dtype)], [], [value])[0]
+def laid_out(values):
+    runs, length, columns = values[0].shape
+
+    def body(*refs):
+        for value, out in zip(refs[: len(values)], refs[len(values) :]):
+            for i in range(runs):
+                out[i * length : (i + 1) * length] = value[i]
+
+    return kernel(body, [((runs * length, columns), f32)] * len(values), [], values)
 
 
 def both_cores(core, keep, got):
@@ -348,13 +352,12 @@
     chosen = jnp.broadcast_to(chosen[:, :, None], (local_runs, length, columns))
     each = length // STRETCHES
     chosen = [
-        chosen[:, part * each : (part + 1) * each].reshape(local_runs * each, columns)
+        chosen[:, part * each : (part + 1) * each]
         for part in range(STRETCHES)
     ]
 
-    chosen[0] = copied(chosen[0])
-
-    matching, pulled[0] = lax.optimization_barrier((matching, pulled[0]))
+    chosen = laid_out(chosen)
+
     other_matching = swap_cores(matching)
     chip_match = jnp.concatenate(
         [

time: 131 us -> 128 us (0.977)
  local copies, waits for them, and re-layouts: 10.6 us -> 4.62 us
  waiting for transfers between devices: 33.9 us -> 38.4 us
  Pallas kernels: 13.9 us -> 11.6 us
  other arithmetic: 0.68 us -> 2.01 us
    unnamed x29 -> x7, local copies, waits for them, and re-layouts: 6.47 us -> 0.67 us
    ppermute x15, waiting for transfers between devices: 19.5 us -> 25 us  [shift_tp(): return lax.ppermute(value, 'tp', along_tp(dx)) if dx % TP else value]
    pallas_call x16, Pallas kernels: 13.9 us -> 11.6 us  [kernel(): return call(*scalars, *arrays)]
  transfers between devices with their start and end apart: 40 -> 40, of which waited for: 18 -> 19; matrix products, arithmetic and copies ran while one was open for 2% -> 3% of each run, Pallas kernels for 10% -> 8%
where the time goes in v1:
time: 128 us
  starting transfers between devices  46 us (36%)
  waiting for transfers between devices  38.4 us (30%)
  blocking collectives  24.4 us (19%)
  Pallas kernels  11.6 us (9%)
  local copies, waits for them, and re-layouts  4.62 us (4%)
  other arithmetic  2.01 us (2%)
    ppermute x15, waiting for transfers between devices, shift_tp(): return lax.ppermute(value, 'tp', along_tp(dx)) if dx % TP else value  25 us
    all_to_all x1, blocking collectives, per_device(): lax.all_to_all(grad, 'runs', 0, 0, axis_index_groups=groups, tiled=True)  24.4 us
    ppermute x15, starting transfers between devices, shift_tp(): return lax.ppermute(value, 'tp', along_tp(dx)) if dx % TP else value  21.2 us
    ppermute x12, starting transfers between devices, by_core(): return lax.ppermute(value, 'runs', pairs)  17.2 us
    pallas_call x16, Pallas kernels, kernel(): return call(*scalars, *arrays)  11.6 us
    ppermute x12, waiting for transfers between devices, by_core(): return lax.ppermute(value, 'runs', pairs)  6.95 us
    ppermute x1, waiting for transfers between devices, per_device(): return (intervened, lax.ppermute(grad, ('runs', 'tp'), home))  6.2 us
    ppermute x3, starting transfers between devices, shift_y(): lax.ppermute(value, 'runs', along_runs(0, dy, 0))  4.42 us
  transfers between devices with their start and end apart: 40, of which 19 were waited for; matrix products, arithmetic and copies ran while one was open for 3% of the time, Pallas kernels for 8%

profile of v1, /device:TPU:6, one launch (start us, length us, event | category | flops | bytes accessed | tf_op | source)
XLA Modules:
  0.0 128.1 jit_solution(8645688886223760537)
XLA Ops:
  0.7 2.4 %dynamic-slice_convert_fusion = (bf16[1024,128]{1,0:T(8,128)(2,1)S(1)}, bf16[1024,128]{1,0:T(8,128)(2,1)}, bf16[1024,128]{1,0:T(8,128)(2,1)}) fusion(f32[8192,128]{1,0:T(8,128)} %param.7, s32[]{:T(128)S(6)} %select_n.216, s32[]{:T(128)S(6)} %select_n.212, s32[]{:T(128)S(6)} %select_n.214), kind=kLoop, calls=%fused_computation.2 | loop fusion | bytes 1572876 | tf_op jit(solution)/shard_map/convert_element_type | solution.py:344
  3.5 1.7 %collective-permute-start.5 = (bf16[1024,128]{1,0:T(8,128)(2,1)}, bf16[1024,128]{1,0:T(8,128)(2,1)S(1)}, u32[]{:S(2)}, u32[]{:S(2)}) collective-permute-start(bf16[1024,128]{1,0:T(8,128)(2,1)} %get-tuple-element.88), channel_id=1, source_target_pairs={{0,3},{1,0},{2,1},{3,2},{4,7},{5,4},{6,5},{7,6},{8,11},{9,8},{10,9... | collective-permute-start | bytes 786440 | tf_op jit(solution)/shard_map/ppermute | solution.py:31
  5.1 1.4 %collective-permute-start.6 = (bf16[1024,128]{1,0:T(8,128)(2,1)S(1)}, bf16[1024,128]{1,0:T(8,128)(2,1)S(1)}, u32[]{:S(2)}, u32[]{:S(2)}) collective-permute-start(bf16[1024,128]{1,0:T(8,128)(2,1)S(1)} %get-tuple-element.86), channel_id=1, source_target_pairs={{0,2},{1,3},{2,0},{3,1},{4,6},{5,7},{6,4},{7,5},{8,10},{9,11},{10,... | collective-permute-start | bytes 786440 | tf_op jit(solution)/shard_map/ppermute | solution.py:31
  6.5 0.7 compare_convert_fusion
  7.2 0.8 multiply_convert_fusion
  8.3 4.2 %collective-permute-done.4.refs_0_.refs_8_ = bf16[1024,128]{1,0:T(8,128)(2,1)S(1)} collective-permute-done((bf16[1024,128]{1,0:T(8,128)(2,1)}, bf16[1024,128]{1,0:T(8,128)(2,1)S(1)}, u32[]{:S(2)}, u32[]{:S(2)}) %collective-permute-start.4) | collective-permute-done | bytes 262176 | tf_op jit(solution)/shard_map/ppermute | solution.py:31
  12.5 1.5 %collective-permute-done.5.refs_1_.refs_10_ = bf16[1024,128]{1,0:T(8,128)(2,1)S(1)} collective-permute-done((bf16[1024,128]{1,0:T(8,128)(2,1)}, bf16[1024,128]{1,0:T(8,128)(2,1)S(1)}, u32[]{:S(2)}, u32[]{:S(2)}) %collective-permute-start.5) | collective-permute-done | bytes 262176 | tf_op jit(solution)/shard_map/ppermute | solution.py:31
  14.0 4.2 %collective-permute-done.6.refs_2_.refs_9_ = bf16[1024,128]{1,0:T(8,128)(2,1)S(1)} collective-permute-done((bf16[1024,128]{1,0:T(8,128)(2,1)S(1)}, bf16[1024,128]{1,0:T(8,128)(2,1)S(1)}, u32[]{:S(2)}, u32[]{:S(2)}) %collective-permute-start.6) | collective-permute-done | bytes 262176 | tf_op jit(solution)/shard_map/ppermute | solution.py:31
  18.2 1.3 %constant_dynamic-slice_fusion.own_ref = f32[2048,128]{1,0:T(8,128)S(1)} fusion(f32[8192,128]{1,0:T(8,128)} %param.7, s32[]{:T(128)S(6)} %select_n.210), kind=kLoop, calls=%fused_computation.50 | loop fusion | bytes 2097156 | tf_op jit(solution)/shard_map/dynamic_slice | solution.py:347
  19.5 1.2 shard_map.68
  20.8 2.3 %shard_map.70 = (bf16[512,128]{1,0:T(8,128)(2,1)S(1)}, bf16[512,128]{1,0:T(8,128)(2,1)S(1)}, bf16[512,128]{1,0:T(8,128)(2,1)S(1)}, bf16[512,128]{1,0:T(8,128)(2,...) custom-call(s32[1]{0:T(128)} %bitcast.core_ref, bf16[512,2048]{1,0:T(8,128)(2,1)S(1)} %copy-done, ...), custom_call_target="tpu_custom_call" | custom-call | flops 1610612736 | tf_op jit(solution)/shard_map/pallas_call | solution.py:68
  23.4 3.8 %collective-permute-start.1 = (s32[8]{0:T(128)S(1)}, s32[8]{0:T(128)S(1)}, u32[]{:S(2)}, u32[]{:S(2)}) collective-permute-start(s32[8]{0:T(128)S(1)} %get-tuple-element.79), channel_id=1, source_target_pairs={{0,24},{4,28},{8,0},{12,4},{16,8},{20,12},{24,16},{28,20},{32,56},... | collective-permute-start | bytes 104 | tf_op jit(solution)/shard_map/ppermute | solution.py:35
  27.2 3.2 %collective-permute-start.25 = (bf16[512,128]{1,0:T(8,128)(2,1)S(1)}, bf16[512,128]{1,0:T(8,128)(2,1)S(1)}, u32[]{:S(2)}, u32[]{:S(2)}) collective-permute-start(bf16[512,128]{1,0:T(8,128)(2,1)S(1)} %get-tuple-element.60), channel_id=1, source_target_pairs={{0,1},{1,2},{2,3},{3,0},{4,5},{5,6},{6,7},{7,4},{8,9},{9,10},{10,1... | collective-permute-start | bytes 393224 | tf_op jit(solution)/shard_map/ppermute | solution.py:31
  30.5 0.7 collective-permute-start.10
  31.2 2.5 %collective-permute-start.11 = (bf16[512,128]{1,0:T(8,128)(2,1)S(1)}, bf16[512,128]{1,0:T(8,128)(2,1)S(1)}, u32[]{:S(2)}, u32[]{:S(2)}) collective-permute-start(bf16[512,128]{1,0:T(8,128)(2,1)S(1)} %get-tuple-element.43), channel_id=1, source_target_pairs={{0,1},{1,2},{2,3},{3,0},{4,5},{5,6},{6,7},{7,4},{8,9},{9,10},{10,1... | collective-permute-start | bytes 393224 | tf_op jit(solution)/shard_map/ppermute | solution.py:31
  33.7 2.2 %collective-permute-start.12 = (bf16[512,128]{1,0:T(8,128)(2,1)S(1)}, bf16[512,128]{1,0:T(8,128)(2,1)S(1)}, u32[]{:S(2)}, u32[]{:S(2)}) collective-permute-start(bf16[512,128]{1,0:T(8,128)(2,1)S(1)} %get-tuple-element.44), channel_id=1, source_target_pairs={{0,2},{1,3},{2,0},{3,1},{4,6},{5,7},{6,4},{7,5},{8,10},{9,11},{10,... | collective-permute-start | bytes 393224 | tf_op jit(solution)/shard_map/ppermute | solution.py:31
  37.2 1.0 collective-permute-done.26.refs_2_
  38.3 2.3 %collective-permute-done.10.refs_0_ = bf16[512,128]{1,0:T(8,128)(2,1)S(1)} collective-permute-done((bf16[512,128]{1,0:T(8,128)(2,1)S(1)}, bf16[512,128]{1,0:T(8,128)(2,1)S(1)}, u32[]{:S(2)}, u32[]{:S(2)}) %collective-permute-start.10) | collective-permute-done | bytes 131104 | tf_op jit(solution)/shard_map/ppermute | solution.py:31
  41.1 0.9 collective-permute-done.12.refs_2_
  42.3 2.0 %collective-permute-start.28 = (bf16[512,128]{1,0:T(8,128)(2,1)S(1)}, bf16[512,128]{1,0:T(8,128)(2,1)S(1)}, u32[]{:S(2)}, u32[]{:S(2)}) collective-permute-start(bf16[512,128]{1,0:T(8,128)(2,1)S(1)} %shard_map.77.refs_0_), channel_id=1, source_target_pairs={{0,32},{8,40},{16,48},{24,56},{32,64},{40,72},{48,80},{56,88},{64,... | collective-permute-start | bytes 393224 | tf_op jit(solution)/shard_map/ppermute | solution.py:40
  44.3 3.6 %collective-permute-start.29 = (bf16[512,128]{1,0:T(8,128)(2,1)S(1)}, bf16[512,128]{1,0:T(8,128)(2,1)S(1)}, u32[]{:S(2)}, u32[]{:S(2)}) collective-permute-start(bf16[512,128]{1,0:T(8,128)(2,1)S(1)} %shard_map.77.refs_0_), channel_id=1, source_target_pairs={{0,64},{8,72},{16,80},{24,88},{32,96},{40,104},{48,112},{56,120},{... | collective-permute-start | bytes 393224 | tf_op jit(solution)/shard_map/ppermute | solution.py:40
  47.9 1.0 collective-permute-start.30
  48.9 1.1 collective-permute-start.14
  50.5 2.3 %collective-permute-start.16 = (bf16[512,128]{1,0:T(8,128)(2,1)S(1)}, bf16[512,128]{1,0:T(8,128)(2,1)S(1)}, u32[]{:S(2)}, u32[]{:S(2)}) collective-permute-start(bf16[512,128]{1,0:T(8,128)(2,1)S(1)} %shard_map.72.refs_0_), channel_id=1, source_target_pairs={{0,96},{8,104},{16,112},{24,120},{32,0},{40,8},{48,16},{56,24},{64... | collective-permute-start | bytes 393224 | tf_op jit(solution)/shard_map/ppermute | solution.py:40
  53.5 2.2 %collective-permute-start.32 = (bf16[512,128]{1,0:T(8,128)(2,1)S(1)}, bf16[512,128]{1,0:T(8,128)(2,1)S(1)}, u32[]{:S(2)}, u32[]{:S(2)}) collective-permute-start(bf16[512,128]{1,0:T(8,128)(2,1)S(1)} %get-tuple-element.67), channel_id=1, source_target_pairs={{0,16},{8,24},{16,0},{24,8},{32,48},{40,56},{48,32},{56,40},{64,80... | collective-permute-start | bytes 393224 | tf_op jit(solution)/shard_map/ppermute | solution.py:40
  55.7 1.1 collective-permute-start.33
  56.8 2.6 %collective-permute-done.16.refs_3_ = bf16[512,128]{1,0:T(8,128)(2,1)S(1)} collective-permute-done((bf16[512,128]{1,0:T(8,128)(2,1)S(1)}, bf16[512,128]{1,0:T(8,128)(2,1)S(1)}, u32[]{:S(2)}, u32[]{:S(2)}) %collective-permute-start.16) | collective-permute-done | bytes 131104 | tf_op jit(solution)/shard_map/ppermute | solution.py:40
  60.1 2.5 %collective-permute-start.18 = (bf16[512,128]{1,0:T(8,128)(2,1)S(1)}, bf16[512,128]{1,0:T(8,128)(2,1)S(1)}, u32[]{:S(2)}, u32[]{:S(2)}) collective-permute-start(bf16[512,128]{1,0:T(8,128)(2,1)S(1)} %get-tuple-element.50), channel_id=1, source_target_pairs={{0,16},{8,24},{16,0},{24,8},{32,48},{40,56},{48,32},{56,40},{64,80... | collective-permute-start | bytes 393224 | tf_op jit(solution)/shard_map/ppermute | solution.py:40
  62.6 0.9 collective-permute-start.19
  64.3 3.4 %collective-permute-done.17.refs_1_ = bf16[512,128]{1,0:T(8,128)(2,1)S(1)} collective-permute-done((bf16[512,128]{1,0:T(8,128)(2,1)S(1)}, bf16[512,128]{1,0:T(8,128)(2,1)S(1)}, u32[]{:S(2)}, u32[]{:S(2)}) %collective-permute-start.17) | collective-permute-done | bytes 131104 | tf_op jit(solution)/shard_map/ppermute | solution.py:40
  67.7 0.9 collective-permute-done.19.refs_3_
  69.4 3.3 %collective-permute-start.35 = (bf16[512,128]{1,0:T(8,128)(2,1)S(1)}, bf16[512,128]{1,0:T(8,128)(2,1)S(1)}, u32[]{:S(2)}, u32[]{:S(2)}) collective-permute-start(bf16[512,128]{1,0:T(8,128)(2,1)S(1)} %shard_map.80.refs_4_), channel_id=1, source_target_pairs={{0,1},{1,2},{2,3},{3,0},{4,5},{5,6},{6,7},{7,4},{8,9},{9,10},{10,1... | collective-permute-start | bytes 393224 | tf_op jit(solution)/shard_map/ppermute | solution.py:31
  72.7 0.9 collective-permute-start.37
  73.7 2.4 %collective-permute-start.21 = (bf16[512,128]{1,0:T(8,128)(2,1)S(1)}, bf16[512,128]{1,0:T(8,128)(2,1)S(1)}, u32[]{:S(2)}, u32[]{:S(2)}) collective-permute-start(bf16[512,128]{1,0:T(8,128)(2,1)S(1)} %shard_map.75.refs_0_), channel_id=1, source_target_pairs={{0,1},{1,2},{2,3},{3,0},{4,5},{5,6},{6,7},{7,4},{8,9},{9,10},{10,1... | collective-permute-start | bytes 393224 | tf_op jit(solution)/shard_map/ppermute | solution.py:31
  76.1 2.3 %collective-permute-start.22 = (bf16[512,128]{1,0:T(8,128)(2,1)S(1)}, bf16[512,128]{1,0:T(8,128)(2,1)S(1)}, u32[]{:S(2)}, u32[]{:S(2)}) collective-permute-start(bf16[512,128]{1,0:T(8,128)(2,1)S(1)} %shard_map.75.refs_0_), channel_id=1, source_target_pairs={{0,2},{1,3},{2,0},{3,1},{4,6},{5,7},{6,4},{7,5},{8,10},{9,11},{10,... | collective-permute-start | bytes 393224 | tf_op jit(solution)/shard_map/ppermute | solution.py:31
  78.4 1.0 collective-permute-done.35.refs_5_
  79.4 1.2 collective-permute-done.36.refs_6_
  80.7 2.1 %collective-permute-done.37.refs_7_ = bf16[512,128]{1,0:T(8,128)(2,1)S(1)} collective-permute-done((bf16[512,128]{1,0:T(8,128)(2,1)S(1)}, bf16[512,128]{1,0:T(8,128)(2,1)S(1)}, u32[]{:S(2)}, u32[]{:S(2)}) %collective-permute-start.37) | collective-permute-done | bytes 131104 | tf_op jit(solution)/shard_map/ppermute | solution.py:31
  82.8 1.8 %collective-permute-done.21.refs_1_ = bf16[512,128]{1,0:T(8,128)(2,1)S(1)} collective-permute-done((bf16[512,128]{1,0:T(8,128)(2,1)S(1)}, bf16[512,128]{1,0:T(8,128)(2,1)S(1)}, u32[]{:S(2)}, u32[]{:S(2)}) %collective-permute-start.21) | collective-permute-done | bytes 131104 | tf_op jit(solution)/shard_map/ppermute | solution.py:31
  84.6 1.8 %collective-permute-done.22.refs_2_ = bf16[512,128]{1,0:T(8,128)(2,1)S(1)} collective-permute-done((bf16[512,128]{1,0:T(8,128)(2,1)S(1)}, bf16[512,128]{1,0:T(8,128)(2,1)S(1)}, u32[]{:S(2)}, u32[]{:S(2)}) %collective-permute-start.22) | collective-permute-done | bytes 131104 | tf_op jit(solution)/shard_map/ppermute | solution.py:31
  86.3 1.8 %collective-permute-done.23.refs_3_ = bf16[512,128]{1,0:T(8,128)(2,1)S(1)} collective-permute-done((bf16[512,128]{1,0:T(8,128)(2,1)S(1)}, bf16[512,128]{1,0:T(8,128)(2,1)S(1)}, u32[]{:S(2)}, u32[]{:S(2)}) %collective-permute-start.23) | collective-permute-done | bytes 131104 | tf_op jit(solution)/shard_map/ppermute | solution.py:31
  88.1 1.3 %shard_map.82 = f32[4096,128]{1,0:T(8,128)S(1)} custom-call(s32[1]{0:T(128)S(6)} %sub.89.core_ref, bf16[512,2048]{1,0:T(8,128)(2,1)S(1)} %copy-done.1, bf16[512,2048]{1,0:T(8,128)(2,1)S(1)} %copy-done, bf16[512,128]{1,0:T(8,128)(2,1)S(1)} %shard_map.75.refs_0_, bf16[512,128]{1,0:T(8,128)(2,1)S(1)} %collective-permute-done.21.refs_1_, ...), custom_call_target="tpu_custom_call" | custom-call | flops 1073741824 | tf_op jit(solution)/shard_map/pallas_call | solution.py:68
  89.5 1.3 %shard_map.81 = f32[4096,128]{1,0:T(8,128)S(1)} custom-call(s32[1]{0:T(128)} %bitcast.core_ref, bf16[512,2048]{1,0:T(8,128)(2,1)S(1)} %copy-done.1, bf16[512,2048]{1,0:T(8,128)(2,1)S(1)} %copy-done, bf16[512,128]{1,0:T(8,128)(2,1)S(1)} %shard_map.75.refs_0_, bf16[512,128]{1,0:T(8,128)(2,1)S(1)} %collective-permute-done.21.refs_1_, ...), custom_call_target="tpu_custom_call" | custom-call | flops 1073741824 | tf_op jit(solution)/shard_map/pallas_call | solution.py:68
  90.8 2.6 %shard_map.83 = bf16[512,2048]{1,0:T(8,128)(2,1)} custom-call(s32[1]{0:T(128)} %bitcast.core_ref, bf16[512,2048]{1,0:T(8,128)(2,1)S(1)} %copy-done, bf16[2048,128]{1,0:T(8,128)(2,1)S(1)} %get-tuple-element.73.own_ref, bf16[512,128]{1,0:T(8,128)(2,1)S(1)} %shard_map.75.refs_0_, bf16[512,128]{1,0:T(8,128)(2,1)S(1)} %collective-permute-done.21.refs_1_, ...), custom_call_target="tpu_custom_call" | custom-call | flops 1073741824 | tf_op jit(solution)/shard_map/pallas_call | solution.py:68
  93.9 24.4 %all_to_all.5 = bf16[16,256,128]{2,1,0:T(8,128)(2,1)S(1)} all-to-all(bf16[16,256,128]{2,1,0:T(8,128)(2,1)S(1)} %bitcast.2), channel_id=1, replica_groups={{0,8,16,24,32,40,48,56,64,72,80,88,96,104,112,120},{4,12,20,28,36,44,52..., dimensions={0} | all-to-all | bytes 2097152 | tf_op jit(solution)/shard_map/all_to_all | solution.py:410
  118.5 2.8 %collective-permute-start.39 = (f32[256,128]{1,0:T(8,128)S(1)}, f32[256,128]{1,0:T(8,128)S(1)}, u32[]{:S(2)}, u32[]{:S(2)}) collective-permute-start(f32[256,128]{1,0:T(8,128)S(1)} %convert_reduce_fusion), channel_id=1, source_target_pairs={{0,0},{1,33},{2,66},{3,99},{4,4},{5,37},{6,70},{7,103},{8,8},{9,41... | collective-permute-start | bytes 393224 | tf_op jit(solution)/shard_map/ppermute | solution.py:419
  121.2 6.2 %collective-permute-done.39 = f32[256,128]{1,0:T(8,128)S(1)} collective-permute-done((f32[256,128]{1,0:T(8,128)S(1)}, f32[256,128]{1,0:T(8,128)S(1)}, u32[]{:S(2)}, u32[]{:S(2)}) %collective-permute-start.39) | collective-permute-done | bytes 131104 | tf_op jit(solution)/shard_map/ppermute | solution.py:419
  127.4 0.7 copy.8
  (72 shorter events, 7.2 us)
Async XLA Ops:
  0.7 18.8 %copy-start = (bf16[512,2048]{1,0:T(8,128)(2,1)S(1)}, bf16[512,2048]{1,0:T(8,128)(2,1)}, u32[]{:S(2)}) copy-start(bf16[512,2048]{1,0:T(8,128)(2,1)} %hidden_ref.9) | copy-start | bytes 6291460
  3.1 9.4 %collective-permute-start.4 = (bf16[1024,128]{1,0:T(8,128)(2,1)}, bf16[1024,128]{1,0:T(8,128)(2,1)S(1)}, u32[]{:S(2)}, u32[]{:S(2)}) collective-permute-start(bf16[1024,128]{1,0:T(8,128)(2,1)} %get-tuple-element.87), channel_id=1, source_target_pairs={{0,1},{1,2},{2,3},{3,0},{4,5},{5,6},{6,7},{7,4},{8,9},{9,10},{10,1... | collective-permute-start | bytes 786440 | tf_op jit(solution)/shard_map/ppermute | solution.py:31
  3.5 10.5 %collective-permute-start.5 = (bf16[1024,128]{1,0:T(8,128)(2,1)}, bf16[1024,128]{1,0:T(8,128)(2,1)S(1)}, u32[]{:S(2)}, u32[]{:S(2)}) collective-permute-start(bf16[1024,128]{1,0:T(8,128)(2,1)} %get-tuple-element.88), channel_id=1, source_target_pairs={{0,3},{1,0},{2,1},{3,2},{4,7},{5,4},{6,5},{7,6},{8,11},{9,8},{10,9... | collective-permute-start | bytes 786440 | tf_op jit(solution)/shard_map/ppermute | solution.py:31
  5.1 13.1 %collective-permute-start.6 = (bf16[1024,128]{1,0:T(8,128)(2,1)S(1)}, bf16[1024,128]{1,0:T(8,128)(2,1)S(1)}, u32[]{:S(2)}, u32[]{:S(2)}) collective-permute-start(bf16[1024,128]{1,0:T(8,128)(2,1)S(1)} %get-tuple-element.86), channel_id=1, source_target_pairs={{0,2},{1,3},{2,0},{3,1},{4,6},{5,7},{6,4},{7,5},{8,10},{9,11},{10,... | collective-permute-start | bytes 786440 | tf_op jit(solution)/shard_map/ppermute | solution.py:31
  6.5 16.7 %collective-permute-start = (s32[4]{0:T(128)}, s32[4]{0:T(128)S(1)}, u32[]{:S(2)}, u32[]{:S(2)}) collective-permute-start(s32[4]{0:T(128)} %param.8), channel_id=1, source_target_pairs={{0,4},{4,0},{8,12},{12,8},{16,20},{20,16},{24,28},{28,24},{32,36},... | collective-permute-start | bytes 56 | tf_op jit(solution)/shard_map/ppermute | solution.py:44
  8.3 11.2 %copy-start.1 = (bf16[512,2048]{1,0:T(8,128)(2,1)S(1)}, bf16[512,2048]{1,0:T(8,128)(2,1)}, u32[]{:S(2)}) copy-start(bf16[512,2048]{1,0:T(8,128)(2,1)} %cotangent_ref.7) | copy-start | bytes 6291460
  12.5 8.3 %collective-permute-start.7 = (bf16[1024,128]{1,0:T(8,128)(2,1)S(1)}, bf16[1024,128]{1,0:T(8,128)(2,1)S(1)}, u32[]{:S(2)}, u32[]{:S(2)}) collective-permute-start(bf16[1024,128]{1,0:T(8,128)(2,1)S(1)} %collective-permute-done.4.refs_0_.refs_8_), channel_id=1, source_target_pairs={{0,4},{4,0},{8,12},{12,8},{16,20},{20,16},{24,28},{28,24},{32,36},... | collective-permute-start | bytes 786440 | tf_op jit(solution)/shard_map/ppermute | solution.py:44
  14.0 6.8 %collective-permute-start.8 = (bf16[1024,128]{1,0:T(8,128)(2,1)S(1)}, bf16[1024,128]{1,0:T(8,128)(2,1)S(1)}, u32[]{:S(2)}, u32[]{:S(2)}) collective-permute-start(bf16[1024,128]{1,0:T(8,128)(2,1)S(1)} %collective-permute-done.5.refs_1_.refs_10_), channel_id=1, source_target_pairs={{0,4},{4,0},{8,12},{12,8},{16,20},{20,16},{24,28},{28,24},{32,36},... | collective-permute-start | bytes 786440 | tf_op jit(solution)/shard_map/ppermute | solution.py:44
  18.2 2.6 %collective-permute-start.9 = (bf16[1024,128]{1,0:T(8,128)(2,1)S(1)}, bf16[1024,128]{1,0:T(8,128)(2,1)S(1)}, u32[]{:S(2)}, u32[]{:S(2)}) collective-permute-start(bf16[1024,128]{1,0:T(8,128)(2,1)S(1)} %collective-permute-done.6.refs_2_.refs_9_), channel_id=1, source_target_pairs={{0,4},{4,0},{8,12},{12,8},{16,20},{20,16},{24,28},{28,24},{32,36},... | collective-permute-start | bytes 786440 | tf_op jit(solution)/shard_map/ppermute | solution.py:44
  20.8 2.4 %copy-start.2 = (s32[4]{0:T(128)S(1)}, s32[4]{0:T(128)}, u32[]{:S(2)}) copy-start(s32[4]{0:T(128)} %param.8) | copy-start | bytes 52
  23.1 10.6 %collective-permute-start.24 = (bf16[512,128]{1,0:T(8,128)(2,1)S(1)}, bf16[512,128]{1,0:T(8,128)(2,1)S(1)}, u32[]{:S(2)}, u32[]{:S(2)}) collective-permute-start(bf16[512,128]{1,0:T(8,128)(2,1)S(1)} %get-tuple-element.59), channel_id=1, source_target_pairs={{0,3},{1,0},{2,1},{3,2},{4,7},{5,4},{6,5},{7,6},{8,11},{9,8},{10,9... | collective-permute-start | bytes 393224 | tf_op jit(solution)/shard_map/ppermute | solution.py:31
  23.4 7.9 %collective-permute-start.1 = (s32[8]{0:T(128)S(1)}, s32[8]{0:T(128)S(1)}, u32[]{:S(2)}, u32[]{:S(2)}) collective-permute-start(s32[8]{0:T(128)S(1)} %get-tuple-element.79), channel_id=1, source_target_pairs={{0,24},{4,28},{8,0},{12,4},{16,8},{20,12},{24,16},{28,20},{32,56},... | collective-permute-start | bytes 104 | tf_op jit(solution)/shard_map/ppermute | solution.py:35
  27.2 9.4 %collective-permute-start.25 = (bf16[512,128]{1,0:T(8,128)(2,1)S(1)}, bf16[512,128]{1,0:T(8,128)(2,1)S(1)}, u32[]{:S(2)}, u32[]{:S(2)}) collective-permute-start(bf16[512,128]{1,0:T(8,128)(2,1)S(1)} %get-tuple-element.60), channel_id=1, source_target_pairs={{0,1},{1,2},{2,3},{3,0},{4,5},{5,6},{6,7},{7,4},{8,9},{9,10},{10,1... | collective-permute-start | bytes 393224 | tf_op jit(solution)/shard_map/ppermute | solution.py:31
  30.4 7.9 %collective-permute-start.26 = (bf16[512,128]{1,0:T(8,128)(2,1)S(1)}, bf16[512,128]{1,0:T(8,128)(2,1)S(1)}, u32[]{:S(2)}, u32[]{:S(2)}) collective-permute-start(bf16[512,128]{1,0:T(8,128)(2,1)S(1)} %get-tuple-element.61), channel_id=1, source_target_pairs={{0,2},{1,3},{2,0},{3,1},{4,6},{5,7},{6,4},{7,5},{8,10},{9,11},{10,... | collective-permute-start | bytes 393224 | tf_op jit(solution)/shard_map/ppermute | solution.py:31
  30.5 10.2 %collective-permute-start.10 = (bf16[512,128]{1,0:T(8,128)(2,1)S(1)}, bf16[512,128]{1,0:T(8,128)(2,1)S(1)}, u32[]{:S(2)}, u32[]{:S(2)}) collective-permute-start(bf16[512,128]{1,0:T(8,128)(2,1)S(1)} %get-tuple-element.42), channel_id=1, source_target_pairs={{0,3},{1,0},{2,1},{3,2},{4,7},{5,4},{6,5},{7,6},{8,11},{9,8},{10,9... | collective-permute-start | bytes 393224 | tf_op jit(solution)/shard_map/ppermute | solution.py:31
  31.2 9.9 %collective-permute-start.11 = (bf16[512,128]{1,0:T(8,128)(2,1)S(1)}, bf16[512,128]{1,0:T(8,128)(2,1)S(1)}, u32[]{:S(2)}, u32[]{:S(2)}) collective-permute-start(bf16[512,128]{1,0:T(8,128)(2,1)S(1)} %get-tuple-element.43), channel_id=1, source_target_pairs={{0,1},{1,2},{2,3},{3,0},{4,5},{5,6},{6,7},{7,4},{8,9},{9,10},{10,1... | collective-permute-start | bytes 393224 | tf_op jit(solution)/shard_map/ppermute | solution.py:31
  33.7 8.3 %collective-permute-start.12 = (bf16[512,128]{1,0:T(8,128)(2,1)S(1)}, bf16[512,128]{1,0:T(8,128)(2,1)S(1)}, u32[]{:S(2)}, u32[]{:S(2)}) collective-permute-start(bf16[512,128]{1,0:T(8,128)(2,1)S(1)} %get-tuple-element.44), channel_id=1, source_target_pairs={{0,2},{1,3},{2,0},{3,1},{4,6},{5,7},{6,4},{7,5},{8,10},{9,11},{10,... | collective-permute-start | bytes 393224 | tf_op jit(solution)/shard_map/ppermute | solution.py:31
  36.5 5.7 %collective-permute-start.2 = (s32[8]{0:T(128)S(1)}, s32[8]{0:T(128)S(1)}, u32[]{:S(2)}, u32[]{:S(2)}) collective-permute-start(s32[8]{0:T(128)S(1)} %get-tuple-element.79), channel_id=1, source_target_pairs={{0,16},{4,20},{8,24},{12,28},{16,0},{20,4},{24,8},{28,12},{32,48},... | collective-permute-start | bytes 104 | tf_op jit(solution)/shard_map/ppermute | solution.py:35
  38.2 11.7 %collective-permute-start.3 = (s32[8]{0:T(128)S(1)}, s32[8]{0:T(128)S(1)}, u32[]{:S(2)}, u32[]{:S(2)}) collective-permute-start(s32[8]{0:T(128)S(1)} %get-tuple-element.79), channel_id=1, source_target_pairs={{0,8},{4,12},{8,16},{12,20},{16,24},{20,28},{24,0},{28,4},{32,40},... | collective-permute-start | bytes 104 | tf_op jit(solution)/shard_map/ppermute | solution.py:35
  40.6 1.6 %collective-permute-start.27 = (bf16[256,128]{1,0:T(8,128)(2,1)S(1)}, bf16[256,128]{1,0:T(8,128)(2,1)S(1)}, u32[]{:S(2)}, u32[]{:S(2)}) collective-permute-start(bf16[256,128]{1,0:T(8,128)(2,1)S(1)} %get-tuple-element.63), channel_id=1, source_target_pairs={{0,4},{4,0},{8,12},{12,8},{16,20},{20,16},{24,28},{28,24},{32,36},... | collective-permute-start | bytes 196616 | tf_op jit(solution)/shard_map/ppermute | solution.py:44
  42.1 6.7 %collective-permute-start.13 = (bf16[256,128]{1,0:T(8,128)(2,1)S(1)}, bf16[256,128]{1,0:T(8,128)(2,1)S(1)}, u32[]{:S(2)}, u32[]{:S(2)}) collective-permute-start(bf16[256,128]{1,0:T(8,128)(2,1)S(1)} %get-tuple-element.46), channel_id=1, source_target_pairs={{0,4},{4,0},{8,12},{12,8},{16,20},{20,16},{24,28},{28,24},{32,36},... | collective-permute-start | bytes 196616 | tf_op jit(solution)/shard_map/ppermute | solution.py:44
  42.3 8.3 %collective-permute-start.28 = (bf16[512,128]{1,0:T(8,128)(2,1)S(1)}, bf16[512,128]{1,0:T(8,128)(2,1)S(1)}, u32[]{:S(2)}, u32[]{:S(2)}) collective-permute-start(bf16[512,128]{1,0:T(8,128)(2,1)S(1)} %shard_map.77.refs_0_), channel_id=1, source_target_pairs={{0,32},{8,40},{16,48},{24,56},{32,64},{40,72},{48,80},{56,88},{64,... | collective-permute-start | bytes 393224 | tf_op jit(solution)/shard_map/ppermute | solution.py:40
  44.3 8.5 %collective-permute-start.29 = (bf16[512,128]{1,0:T(8,128)(2,1)S(1)}, bf16[512,128]{1,0:T(8,128)(2,1)S(1)}, u32[]{:S(2)}, u32[]{:S(2)}) collective-permute-start(bf16[512,128]{1,0:T(8,128)(2,1)S(1)} %shard_map.77.refs_0_), channel_id=1, source_target_pairs={{0,64},{8,72},{16,80},{24,88},{32,96},{40,104},{48,112},{56,120},{... | collective-permute-start | bytes 393224 | tf_op jit(solution)/shard_map/ppermute | solution.py:40
  47.9 5.0 %collective-permute-start.30 = (bf16[512,128]{1,0:T(8,128)(2,1)S(1)}, bf16[512,128]{1,0:T(8,128)(2,1)S(1)}, u32[]{:S(2)}, u32[]{:S(2)}) collective-permute-start(bf16[512,128]{1,0:T(8,128)(2,1)S(1)} %shard_map.77.refs_0_), channel_id=1, source_target_pairs={{0,96},{8,104},{16,112},{24,120},{32,0},{40,8},{48,16},{56,24},{64... | collective-permute-start | bytes 393224 | tf_op jit(solution)/shard_map/ppermute | solution.py:40
  48.9 6.9 %collective-permute-start.14 = (bf16[512,128]{1,0:T(8,128)(2,1)S(1)}, bf16[512,128]{1,0:T(8,128)(2,1)S(1)}, u32[]{:S(2)}, u32[]{:S(2)}) collective-permute-start(bf16[512,128]{1,0:T(8,128)(2,1)S(1)} %shard_map.72.refs_0_), channel_id=1, source_target_pairs={{0,32},{8,40},{16,48},{24,56},{32,64},{40,72},{48,80},{56,88},{64,... | collective-permute-start | bytes 393224 | tf_op jit(solution)/shard_map/ppermute | solution.py:40
  50.1 6.8 %collective-permute-start.15 = (bf16[512,128]{1,0:T(8,128)(2,1)S(1)}, bf16[512,128]{1,0:T(8,128)(2,1)S(1)}, u32[]{:S(2)}, u32[]{:S(2)}) collective-permute-start(bf16[512,128]{1,0:T(8,128)(2,1)S(1)} %shard_map.72.refs_0_), channel_id=1, source_target_pairs={{0,64},{8,72},{16,80},{24,88},{32,96},{40,104},{48,112},{56,120},{... | collective-permute-start | bytes 393224 | tf_op jit(solution)/shard_map/ppermute | solution.py:40
  50.5 8.9 %collective-permute-start.16 = (bf16[512,128]{1,0:T(8,128)(2,1)S(1)}, bf16[512,128]{1,0:T(8,128)(2,1)S(1)}, u32[]{:S(2)}, u32[]{:S(2)}) collective-permute-start(bf16[512,128]{1,0:T(8,128)(2,1)S(1)} %shard_map.72.refs_0_), channel_id=1, source_target_pairs={{0,96},{8,104},{16,112},{24,120},{32,0},{40,8},{48,16},{56,24},{64... | collective-permute-start | bytes 393224 | tf_op jit(solution)/shard_map/ppermute | solution.py:40
  53.5 9.1 %collective-permute-start.31 = (bf16[512,128]{1,0:T(8,128)(2,1)S(1)}, bf16[512,128]{1,0:T(8,128)(2,1)S(1)}, u32[]{:S(2)}, u32[]{:S(2)}) collective-permute-start(bf16[512,128]{1,0:T(8,128)(2,1)S(1)} %get-tuple-element.66), channel_id=1, source_target_pairs={{0,8},{8,16},{16,24},{24,0},{32,40},{40,48},{48,56},{56,32},{64,72... | collective-permute-start | bytes 393224 | tf_op jit(solution)/shard_map/ppermute | solution.py:40
  53.5 10.0 %collective-permute-start.32 = (bf16[512,128]{1,0:T(8,128)(2,1)S(1)}, bf16[512,128]{1,0:T(8,128)(2,1)S(1)}, u32[]{:S(2)}, u32[]{:S(2)}) collective-permute-start(bf16[512,128]{1,0:T(8,128)(2,1)S(1)} %get-tuple-element.67), channel_id=1, source_target_pairs={{0,16},{8,24},{16,0},{24,8},{32,48},{40,56},{48,32},{56,40},{64,80... | collective-permute-start | bytes 393224 | tf_op jit(solution)/shard_map/ppermute | solution.py:40
  55.7 7.8 %collective-permute-start.33 = (bf16[512,128]{1,0:T(8,128)(2,1)S(1)}, bf16[512,128]{1,0:T(8,128)(2,1)S(1)}, u32[]{:S(2)}, u32[]{:S(2)}) collective-permute-start(bf16[512,128]{1,0:T(8,128)(2,1)S(1)} %get-tuple-element.68), channel_id=1, source_target_pairs={{0,24},{8,0},{16,8},{24,16},{32,56},{40,32},{48,40},{56,48},{64,88... | collective-permute-start | bytes 393224 | tf_op jit(solution)/shard_map/ppermute | solution.py:40
  60.0 7.7 %collective-permute-start.17 = (bf16[512,128]{1,0:T(8,128)(2,1)S(1)}, bf16[512,128]{1,0:T(8,128)(2,1)S(1)}, u32[]{:S(2)}, u32[]{:S(2)}) collective-permute-start(bf16[512,128]{1,0:T(8,128)(2,1)S(1)} %get-tuple-element.49), channel_id=1, source_target_pairs={{0,8},{8,16},{16,24},{24,0},{32,40},{40,48},{48,56},{56,32},{64,72... | collective-permute-start | bytes 393224 | tf_op jit(solution)/shard_map/ppermute | solution.py:40
  60.1 7.6 %collective-permute-start.18 = (bf16[512,128]{1,0:T(8,128)(2,1)S(1)}, bf16[512,128]{1,0:T(8,128)(2,1)S(1)}, u32[]{:S(2)}, u32[]{:S(2)}) collective-permute-start(bf16[512,128]{1,0:T(8,128)(2,1)S(1)} %get-tuple-element.50), channel_id=1, source_target_pairs={{0,16},{8,24},{16,0},{24,8},{32,48},{40,56},{48,32},{56,40},{64,80... | collective-permute-start | bytes 393224 | tf_op jit(solution)/shard_map/ppermute | solution.py:40
  62.6 6.0 %collective-permute-start.19 = (bf16[512,128]{1,0:T(8,128)(2,1)S(1)}, bf16[512,128]{1,0:T(8,128)(2,1)S(1)}, u32[]{:S(2)}, u32[]{:S(2)}) collective-permute-start(bf16[512,128]{1,0:T(8,128)(2,1)S(1)} %get-tuple-element.51), channel_id=1, source_target_pairs={{0,24},{8,0},{16,8},{24,16},{32,56},{40,32},{48,40},{56,48},{64,88... | collective-permute-start | bytes 393224 | tf_op jit(solution)/shard_map/ppermute | solution.py:40
  64.2 5.2 %collective-permute-start.34 = (f32[256,128]{1,0:T(8,128)S(1)}, f32[256,128]{1,0:T(8,128)S(1)}, u32[]{:S(2)}, u32[]{:S(2)}) collective-permute-start(f32[256,128]{1,0:T(8,128)S(1)} %get-tuple-element.70), channel_id=1, source_target_pairs={{0,4},{4,0},{8,12},{12,8},{16,20},{20,16},{24,28},{28,24},{32,36},... | collective-permute-start | bytes 393224 | tf_op jit(solution)/shard_map/ppermute | solution.py:44
  69.2 4.5 %collective-permute-start.20 = (f32[256,128]{1,0:T(8,128)S(1)}, f32[256,128]{1,0:T(8,128)S(1)}, u32[]{:S(2)}, u32[]{:S(2)}) collective-permute-start(f32[256,128]{1,0:T(8,128)S(1)} %get-tuple-element.53), channel_id=1, source_target_pairs={{0,4},{4,0},{8,12},{12,8},{16,20},{20,16},{24,28},{28,24},{32,36},... | collective-permute-start | bytes 393224 | tf_op jit(solution)/shard_map/ppermute | solution.py:44
  69.4 10.0 %collective-permute-start.35 = (bf16[512,128]{1,0:T(8,128)(2,1)S(1)}, bf16[512,128]{1,0:T(8,128)(2,1)S(1)}, u32[]{:S(2)}, u32[]{:S(2)}) collective-permute-start(bf16[512,128]{1,0:T(8,128)(2,1)S(1)} %shard_map.80.refs_4_), channel_id=1, source_target_pairs={{0,1},{1,2},{2,3},{3,0},{4,5},{5,6},{6,7},{7,4},{8,9},{9,10},{10,1... | collective-permute-start | bytes 393224 | tf_op jit(solution)/shard_map/ppermute | solution.py:31
  72.7 7.9 %collective-permute-start.36 = (bf16[512,128]{1,0:T(8,128)(2,1)S(1)}, bf16[512,128]{1,0:T(8,128)(2,1)S(1)}, u32[]{:S(2)}, u32[]{:S(2)}) collective-permute-start(bf16[512,128]{1,0:T(8,128)(2,1)S(1)} %shard_map.80.refs_4_), channel_id=1, source_target_pairs={{0,2},{1,3},{2,0},{3,1},{4,6},{5,7},{6,4},{7,5},{8,10},{9,11},{10,... | collective-permute-start | bytes 393224 | tf_op jit(solution)/shard_map/ppermute | solution.py:31
  72.7 10.1 %collective-permute-start.37 = (bf16[512,128]{1,0:T(8,128)(2,1)S(1)}, bf16[512,128]{1,0:T(8,128)(2,1)S(1)}, u32[]{:S(2)}, u32[]{:S(2)}) collective-permute-start(bf16[512,128]{1,0:T(8,128)(2,1)S(1)} %shard_map.80.refs_4_), channel_id=1, source_target_pairs={{0,3},{1,0},{2,1},{3,2},{4,7},{5,4},{6,5},{7,6},{8,11},{9,8},{10,9... | collective-permute-start | bytes 393224 | tf_op jit(solution)/shard_map/ppermute | solution.py:31
  73.7 10.8 %collective-permute-start.21 = (bf16[512,128]{1,0:T(8,128)(2,1)S(1)}, bf16[512,128]{1,0:T(8,128)(2,1)S(1)}, u32[]{:S(2)}, u32[]{:S(2)}) collective-permute-start(bf16[512,128]{1,0:T(8,128)(2,1)S(1)} %shard_map.75.refs_0_), channel_id=1, source_target_pairs={{0,1},{1,2},{2,3},{3,0},{4,5},{5,6},{6,7},{7,4},{8,9},{9,10},{10,1... | collective-permute-start | bytes 393224 | tf_op jit(solution)/shard_map/ppermute | solution.py:31
  76.1 10.2 %collective-permute-start.22 = (bf16[512,128]{1,0:T(8,128)(2,1)S(1)}, bf16[512,128]{1,0:T(8,128)(2,1)S(1)}, u32[]{:S(2)}, u32[]{:S(2)}) collective-permute-start(bf16[512,128]{1,0:T(8,128)(2,1)S(1)} %shard_map.75.refs_0_), channel_id=1, source_target_pairs={{0,2},{1,3},{2,0},{3,1},{4,6},{5,7},{6,4},{7,5},{8,10},{9,11},{10,... | collective-permute-start | bytes 393224 | tf_op jit(solution)/shard_map/ppermute | solution.py:31
  79.4 8.7 %collective-permute-start.23 = (bf16[512,128]{1,0:T(8,128)(2,1)S(1)}, bf16[512,128]{1,0:T(8,128)(2,1)S(1)}, u32[]{:S(2)}, u32[]{:S(2)}) collective-permute-start(bf16[512,128]{1,0:T(8,128)(2,1)S(1)} %shard_map.75.refs_0_), channel_id=1, source_target_pairs={{0,3},{1,0},{2,1},{3,2},{4,7},{5,4},{6,5},{7,6},{8,11},{9,8},{10,9... | collective-permute-start | bytes 393224 | tf_op jit(solution)/shard_map/ppermute | solution.py:31
  89.4 4.2 %collective-permute-start.38 = (f32[4096,128]{1,0:T(8,128)S(1)}, f32[4096,128]{1,0:T(8,128)S(1)}, u32[]{:S(2)}, u32[]{:S(2)}) collective-permute-start(f32[4096,128]{1,0:T(8,128)S(1)} %shard_map.82), channel_id=1, source_target_pairs={{0,4},{4,0},{8,12},{12,8},{16,20},{20,16},{24,28},{28,24},{32,36},... | collective-permute-start | bytes 6291464 | tf_op jit(solution)/shard_map/ppermute | solution.py:44
  118.5 9.0 %collective-permute-start.39 = (f32[256,128]{1,0:T(8,128)S(1)}, f32[256,128]{1,0:T(8,128)S(1)}, u32[]{:S(2)}, u32[]{:S(2)}) collective-permute-start(f32[256,128]{1,0:T(8,128)S(1)} %convert_reduce_fusion), channel_id=1, source_target_pairs={{0,0},{1,33},{2,66},{3,99},{4,4},{5,37},{6,70},{7,103},{8,8},{9,41... | collective-permute-start | bytes 393224 | tf_op jit(solution)/shard_map/ppermute | solution.py:419
